TPU v7x, 32 devices: a whole 2x2x4 slice. The times are simulated.
32 devices in a mesh: curve: 16 (over z, y, x), group: 2 (over core).
Axes of the slice: x: 2, y: 2, z: 4, core: 2. Of those that a mesh axis runs over, the one named last changes fastest.
Arguments:
- particles: float32 [512, 9, 128], P(('curve', 'group')), may hold values from -2 to 8, as said below
- counts: int32 [512], P(('curve', 'group')), may hold values from 16 to 128
- pair_lists: int32 [512, 13], P(('curve', 'group')), may hold values from -1 to 511, as said below
Outputs:
- density: float32 [512, 128], P(('curve', 'group'))
- acceleration: float32 [512, 3, 128], P(('curve', 'group'))
Inputs may be any that keep to these rules, and one draw needn't show every extreme that they name: `particles`: the position of every slot of a cell lies in that cell's own unit box of the grid; channels 6, 7 and 8 are positive in every slot. `pair_lists`: the entries of row i other than -1 are distinct cells among i - 8 * 8 + 1 to i + 2 * 8 * 8 - 1, none equal to i, and no cell is named twice in one column.
All inputs are finite; a program needn't handle non-finite values.
Results may differ from a plain program's by a relative error of at most 0.0003.
Values sent between devices are 32-bit elements; how exact they have to be, the bound alone decides.
No kernel may reach another device: no remote copies, remote signals or barrier semaphores. Data moves between devices by JAX's collectives and lax.ppermute only.
A program may use at most 128 MiB of HBM per device.

v0:
```python
import jax
import jax.numpy as jnp
from jax import lax
from jax.experimental import pallas as pl
from jax.experimental.pallas import tpu as pltpu
from jax.sharding import PartitionSpec as P


FARTHEST = 127

gamma_index = 5.0 / 3.0
kernel_norm = 21.0 / (2.0 * 3.141592653589793)
slope_norm = 105.0 / (2.0 * 3.141592653589793)

LANES = 128
ROOM = 12 << 20
TINY = 1.2e-38
AXES = ("curve", "group")


def swap_cores(block):
    return lax.ppermute(block, "group", [(0, 1), (1, 0)])


def reach_of(local_cells):
    return -(-FARTHEST // (2 * local_cells))


def route_of(chips, k):
    route = []
    for chip in range(chips):
        route.append((2 * (chip + k) if chip + k < chips else 2 * chip + 1, 2 * chip))
        route.append((2 * (chip - k) + 1 if chip - k >= 0 else 2 * chip, 2 * chip + 1))
    return route


def surround(block, beside):
    chips = lax.axis_size("curve")
    chip_block = jnp.concatenate([block, swap_cores(block)], axis=0)
    reach = reach_of(block.shape[0])
    fetched = []
    for k in range(1, reach + 1):
        fetched.append(lax.ppermute(chip_block, AXES, route_of(chips, k)))
    made = beside(chip_block)
    fetched = jnp.concatenate(fetched, axis=0)
    return jnp.concatenate([chip_block, fetched, swap_cores(fetched)], axis=0), made


def window_starts(chip, core, local_cells, reach):
    side = 1 - 2 * core
    runs = [(chip, core), (chip, 1 - core)]
    for k in range(1, reach + 1):
        runs += [(chip + side * k, core), (chip + side * k, 1 - core)]
    for k in range(1, reach + 1):
        runs += [(chip - side * k, 1 - core), (chip - side * k, core)]
    return [((2 * where + half) * local_cells, where) for where, half in runs]


def pack_sources(cell, codes_ref, columns, tables, packs, pad_tiles):
    lane = lax.broadcasted_iota(jnp.int32, (1, LANES), 1)
    held = [jnp.zeros(pack.shape[1:], jnp.float32) for pack in packs]
    place = jnp.int32(0)
    for entry in range(2 * columns + 1):
        code = codes_ref[cell, entry]
        row = lax.shift_right_logical(code, 8)
        count = lax.bitwise_and(code, 255)
        tile = lax.shift_right_logical(place, 7)
        turn = lax.bitwise_and(place, 127)
        place = place + count
        crossed = lax.shift_right_logical(place, 7) > tile
        beyond = lane >= turn
        for n, (table, pack) in enumerate(zip(tables, packs)):
            rolled = pltpu.roll(table[row], turn, 1)
            merged = jnp.where(beyond, rolled, held[n])
            pack[tile] = merged
            held[n] = jnp.where(crossed, rolled, merged)
    tile = lax.shift_right_logical(place, 7)
    inside = lane < lax.bitwise_and(place, 127)
    for n, pack in enumerate(packs):
        pack[tile] = jnp.where(inside, held[n], 0.0)
        for extra in range(1, pad_tiles):
            pack[tile + extra] = jnp.zeros(pack.shape[1:], jnp.float32)
    return lax.shift_right_logical(place + 127, 7)


def each_group(count, tile_count, body, finish, zeros):
    fours = lax.shift_right_logical(tile_count + 1, 2)
    twos = jnp.where(tile_count > 4 * fours, 1, 0)

    def per_group(start, rows):
        span = pl.ds(pl.multiple_of(start, 8), rows)
        step = body(span)
        total = zeros(rows)
        total = lax.fori_loop(0, fours, lambda k, t: step(4 * k, 4, t), total)
        total = lax.fori_loop(0, twos, lambda k, t: step(4 * fours, 2, t), total)
        finish(span, total)

    def whole(group, carry):
        per_group(group * 16, 16)
        return carry

    eights = lax.shift_right_logical(count + 7, 3)
    wholes = lax.shift_right_logical(eights, 1)
    lax.fori_loop(0, wholes, whole, 0)

    def rest(_, carry):
        per_group(wholes * 16, 8)
        return carry

    lax.fori_loop(0, lax.bitwise_and(eights, 1), rest, 0)


def row_sums(sums, local_cells):
    lane = lax.broadcasted_iota(jnp.int32, (LANES, LANES), 1)
    held = jnp.zeros((LANES, LANES), jnp.float32)
    for cell in range(local_cells):
        held = jnp.where(lane == cell, jnp.sum(sums[cell], axis=1, keepdims=True), held)
    return jnp.transpose(held)[:local_cells]


def prepare_kernel(counts_ref, particles_ref, lists_ref, sent_ref, padded_ref, own_ref):
    local_cells, columns = lists_ref.shape
    lane = lax.broadcasted_iota(jnp.int32, (1, LANES), 1)
    padded_ref[...] = jnp.full(padded_ref.shape, -1, jnp.int32)
    padded_ref[:, 0:columns] = lists_ref[...]
    for cell in range(local_cells):
        count = counts_ref[cell]
        row = slice(cell, cell + 1)
        for c, d in enumerate((0, 1, 2, None, 3, 4, 5)):
            if d is not None:
                sent_ref[cell, c : c + 1, :] = particles_ref[d, row, :]
        sent_ref[cell, 3:4, :] = jnp.where(lane < count, particles_ref[7, row, :], 0.0)
        sent_ref[cell, 7:8, :] = ((padded_ref[row, :] + 1) * 256 + count).astype(jnp.float32)
    smooth = particles_ref[6]
    steep = slope_norm ** (1.0 / 3.0) * jnp.exp((-5.0 / 3.0) * jnp.log(smooth))
    rows = [particles_ref[d] for d in range(6)] + [2.0 / smooth, smooth * 0.05, steep, steep * (0.5 / smooth)]
    for cell in range(local_cells):
        for c, row in enumerate(rows):
            own_ref[cell, c : c + 1, :] = row[cell : cell + 1]


def spread_kernel(rows_ref, after_ref, spread_ref):
    def per_pair(pair, carry):
        cells = (2 * pair, 2 * pair + 1)
        held = [jnp.transpose(rows_ref[cell]) for cell in cells]
        for c in range(spread_ref.shape[1]):
            for cell, columns in zip(cells, held):
                spread_ref[cell, c] = jnp.broadcast_to(columns[:, c : c + 1], (LANES, LANES))
        return carry

    lax.fori_loop(0, spread_ref.shape[0] // 2, per_pair, 0)


def partner_codes(place_ref, padded_ref, table_ref, code_ref, listed_ref, found_ref, columns, chips):
    local_cells = padded_ref.shape[0]
    reach = reach_of(local_cells)
    lane = lax.broadcasted_iota(jnp.int32, (1, LANES), 1)
    inner = lax.broadcasted_iota(jnp.int32, (8, LANES), 0)
    starts = window_starts(place_ref[0], place_ref[1], local_cells, reach)
    groups = []
    for first in range(0, table_ref.shape[0], 8):
        start, where = starts[first // local_cells]
        span = slice(first, first + 8)
        lists = table_ref[span, 7, :].astype(jnp.int32)
        real = (where >= 0) & (where < chips)
        count = lax.bitwise_and(lists, 255)
        code_ref[span, :] = jnp.where(real, (inner + first) * 256 + count, 0).astype(jnp.float32)
        listed_ref[span, :] = (lax.shift_right_logical(lists, 8) - 1).astype(jnp.float32)
        groups.append((span, start + first % local_cells))
    own_start = starts[0][0]

    def per_cell(cell, carry):
        own = own_start + cell
        row = padded_ref[pl.ds(cell, 1), :]
        wanted = jnp.where(lane == columns, own, jnp.where(row >= 0, row, -(1 << 20)))
        ahead = jnp.zeros((8, LANES), jnp.float32)
        behind = jnp.zeros((8, LANES), jnp.float32)
        for span, start in groups:
            code = code_ref[span, :]
            ahead = jnp.maximum(ahead, jnp.where(inner == wanted - start, code, 0.0))
            behind = jnp.maximum(behind, jnp.where(listed_ref[span, :] == own.astype(jnp.float32), code, 0.0))
        ahead = jnp.max(ahead, axis=0, keepdims=True)
        behind = pltpu.roll(jnp.max(behind, axis=0, keepdims=True), columns + 1, 1)
        found_ref[pl.ds(cell, 1), :] = jnp.where(lane <= columns, ahead, behind).astype(jnp.int32)
        return carry

    lax.fori_loop(0, local_cells, per_cell, 0)


def density_kernel(
    place_ref, counts_ref, padded_ref, table_ref, particles_ref, own_ref, spread_ref,
    out_ref, state_ref, pack_ref, codes_ref, sums_ref, code_ref, listed_ref, found_ref, *, columns, chips,
):
    local_cells = particles_ref.shape[1]
    partner_codes(place_ref, padded_ref, table_ref, code_ref, listed_ref, found_ref, columns, chips)
    pltpu.sync_copy(found_ref, codes_ref)

    def per_cell(cell, carry):
        tile_count = pack_sources(cell, codes_ref, columns, [table_ref], [pack_ref.at[cell]], 2)

        def body(span):
            xa, ya, za, ia = (spread_ref[cell, c, span, :] for c in (0, 1, 2, 6))

            def step(first, tiles, total):
                for u in range(tiles):
                    at = first + u
                    dx = xa - pack_ref[cell, at, 0:1, :]
                    dy = ya - pack_ref[cell, at, 1:2, :]
                    dz = za - pack_ref[cell, at, 2:3, :]
                    squared = dx * dx + dy * dy + dz * dz
                    scaled = squared * lax.rsqrt(jnp.maximum(squared, TINY)) * ia
                    remain = jnp.maximum(4.0 - scaled, 0.0)
                    remain = remain * remain
                    total = total + remain * remain * ((1.0 + scaled) * pack_ref[cell, at, 3:4, :])
                return total

            return step

        def finish(span, total):
            sums_ref[cell, span, :] = total

        each_group(counts_ref[cell], tile_count, body, finish, lambda rows: jnp.zeros((rows, LANES), jnp.float32))
        return carry

    lax.fori_loop(0, local_cells, per_cell, 0)
    raw = row_sums(sums_ref, local_cells)
    masses = jnp.concatenate([table_ref[cell, 3:4, :] for cell in range(local_cells)], axis=0)
    smooth, entropy = particles_ref[6], particles_ref[8]
    held = masses > 0.0
    smooth = jnp.where(held, smooth, 1.0)
    density = jnp.where(held, raw * (kernel_norm / 256.0) / (smooth * smooth * smooth), 0.0)
    out_ref[...] = density
    bounded = jnp.where(held, density, 1.0)
    log_density = jnp.log(bounded)
    pressure_term = entropy * jnp.exp((gamma_index - 2.0) * log_density)
    sound = jnp.sqrt(gamma_index * entropy * jnp.exp((gamma_index - 1.0) * log_density))
    rows = (bounded * 0.005, pressure_term, sound * 0.025)
    for cell in range(local_cells):
        for c, row in enumerate(rows):
            state_ref[cell, c : c + 1, :] = row[cell : cell + 1]
        state_ref[cell, 3:6, :] = own_ref[cell, 7:10, :]
        state_ref[cell, 6:8, :] = jnp.zeros((2, LANES), jnp.float32)


def force_kernel(
    counts_ref, codes_ref, table_ref, state_ref, pack_ref, spread_ref, state_spread_ref,
    out_ref, state_pack_ref, sums_ref, *, columns,
):
    local_cells = out_ref.shape[1]

    def per_cell(cell, carry):
        tile_count = pack_sources(cell, codes_ref, columns, [state_ref], [state_pack_ref], 2)

        def body(span):
            def step(first, tiles, total):
                for u in range(tiles):
                    at = first + u
                    xa, ya, za, ua, va, wa = (spread_ref[cell, c, span, :] for c in range(6))
                    ga, sa, ja = (spread_ref[cell, c, span, :] for c in range(7, 10))
                    ra, fa, ca = (state_spread_ref[cell, c, span, :] for c in range(3))
                    xb, yb, zb, mb, ub, vb, wb = (pack_ref[cell, at, c : c + 1, :] for c in range(7))
                    rb, fb, cb, gb, sb, jb = (state_pack_ref[at, c : c + 1, :] for c in range(6))
                    dx, dy, dz = xa - xb, ya - yb, za - zb
                    squared = dx * dx + dy * dy + dz * dz
                    apart = squared * lax.rsqrt(jnp.maximum(squared, TINY))
                    closing = (ua - ub) * dx + (va - vb) * dy + (wa - wb) * dz
                    slope_a = jnp.maximum(sa - apart * ja, 0.0)
                    slope_a = slope_a * slope_a * slope_a
                    slope_b = jnp.maximum(sb - apart * jb, 0.0)
                    slope_b = slope_b * slope_b * slope_b
                    width = ga + gb
                    approach = jnp.minimum(width * closing, 0.0) / (squared + width * width)
                    viscous = approach * (approach - (ca + cb)) / (ra + rb)
                    coupling = ((fa + viscous) * slope_a + (fb + viscous) * slope_b) * mb
                    total = (total[0] + coupling * dx, total[1] + coupling * dy, total[2] + coupling * dz)
                return total

            return step

        def finish(span, total):
            for d in range(3):
                sums_ref[d, cell, span, :] = total[d]

        each_group(
            counts_ref[cell], tile_count, body, finish, lambda rows: (jnp.zeros((rows, LANES), jnp.float32),) * 3
        )
        return carry

    lax.fori_loop(0, local_cells, per_cell, 0)
    held = jnp.concatenate([table_ref[cell, 3:4, :] for cell in range(local_cells)], axis=0) > 0.0
    for d in range(3):
        out_ref[d] = jnp.where(held, row_sums(sums_ref.at[d], local_cells), 0.0)


def on_chip(array):
    return pltpu.with_memory_space_constraint(array, pltpu.VMEM)


def per_device(particles, counts, pair_lists):
    local_cells, _, slots = particles.shape
    columns = pair_lists.shape[1]
    assert slots == LANES and local_cells % 8 == 0
    scalars = pl.BlockSpec(memory_space=pltpu.SMEM)
    whole = pl.BlockSpec(memory_space=pltpu.VMEM)
    plain = lambda *shape: jax.ShapeDtypeStruct(shape, jnp.float32)
    floats = lambda *shape: pltpu.VMEM(shape, jnp.float32)
    chips = lax.axis_size("curve")
    place = jnp.stack([lax.axis_index("curve"), lax.axis_index("group")]).astype(jnp.int32)
    particles = jnp.transpose(particles, (1, 0, 2))
    sent, padded, own = pl.pallas_call(
        prepare_kernel,
        out_shape=(plain(local_cells, 8, slots), pltpu.VMEM((local_cells, LANES), jnp.int32), floats(local_cells, 16, slots)),
        in_specs=[scalars, whole, whole],
        out_specs=(whole, whole, whole),
        name="prepare",
        compiler_params=pltpu.CompilerParams(vmem_limit_bytes=ROOM),
    )(counts, particles, pair_lists)

    def spread(rows, channels, after):
        return pl.pallas_call(
            spread_kernel,
            out_shape=floats(local_cells, channels, LANES, LANES),
            in_specs=[whole, pl.BlockSpec(memory_space=pl.ANY)],
            out_specs=whole,
            name="spread",
        compiler_params=pltpu.CompilerParams(vmem_limit_bytes=ROOM),
        )(rows, after)

    window, own_spread = surround(sent, lambda after: spread(own, 10, after))
    table = on_chip(window)
    most_tiles = 2 * columns + 5
    rows = table.shape[0]
    density, state, packed, codes = pl.pallas_call(
        lambda *refs: density_kernel(*refs, columns=columns, chips=chips),
        out_shape=(
            plain(local_cells, slots),
            plain(local_cells, 8, slots),
            floats(local_cells, most_tiles, 8, LANES),
            jax.ShapeDtypeStruct((local_cells, LANES), jnp.int32),
        ),
        in_specs=[scalars, scalars, whole, whole, whole, whole, whole],
        out_specs=(whole, whole, whole, scalars),
        scratch_shapes=[
            floats(local_cells, LANES, LANES),
            floats(rows, LANES),
            floats(rows, LANES),
            pltpu.VMEM((local_cells, LANES), jnp.int32),
        ],
        name="density_sweep",
        compiler_params=pltpu.CompilerParams(vmem_limit_bytes=ROOM),
    )(place, counts, padded, table, particles, own, own_spread)
    states, state_spread = surround(state, lambda after: spread(state, 3, after))
    acceleration = pl.pallas_call(
        lambda *refs: force_kernel(*refs, columns=columns),
        out_shape=plain(3, local_cells, slots),
        in_specs=[scalars, scalars, whole, whole, whole, whole, whole],
        out_specs=whole,
        scratch_shapes=[floats(most_tiles, 8, LANES), floats(3, local_cells, LANES, LANES)],
        name="force_sweep",
        compiler_params=pltpu.CompilerParams(vmem_limit_bytes=ROOM),
    )(counts, codes, table, on_chip(states), packed, own_spread, state_spread)
    return density, jnp.transpose(acceleration, (1, 0, 2))


def solution(mesh):
    in_specs = (P(AXES, None, None), P(AXES), P(AXES, None))
    out_specs = (P(AXES, None), P(AXES, None, None))
    return jax.shard_map(per_device, mesh=mesh, in_specs=in_specs, out_specs=out_specs, check_vma=False)
```

profile of v0, /device:TPU:13, one launch (start us, length us, event | category | flops | bytes accessed | tf_op | source)
XLA Modules:
  0.0 84.4 jit_solution(6659756759032434385)
XLA Ops:
  0.6 0.0 copy-start
  0.6 0.9 %copy-done = f32[16,9,128]{2,0,1:T(8,128)S(1)} copy-done((f32[16,9,128]{2,0,1:T(8,128)S(1)}, f32[16,9,128]{2,0,1:T(8,128)}, u32[]{:S(2)}) %copy-start) | copy-done | bytes 73752
  1.5 0.0 copy-start.2
  1.5 0.7 copy-done.2
  2.2 0.0 copy-start.3
  2.2 0.7 copy-done.3
  2.9 0.6 prepare.1
  3.5 0.7 collective-permute-start
  4.3 0.9 %collective-permute-done = f32[16,8,128]{2,1,0:T(8,128)S(1)} collective-permute-done((f32[16,8,128]{2,1,0:T(8,128)S(1)}, f32[16,8,128]{2,1,0:T(8,128)S(1)}, u32[]{:S(2)}, u32[]{:S(2)}) %collective-permute-start) | collective-permute-done | bytes 65568 | tf_op jit(solution)/shard_map/ppermute | solution.py:22
  5.2 1.3 %collective-permute-start.4 = (f32[32,8,128]{2,1,0:T(8,128)S(1)}, f32[32,8,128]{2,1,0:T(8,128)S(1)}, u32[]{:S(2)}, u32[]{:S(2)}) collective-permute-start(f32[32,8,128]{2,1,0:T(8,128)S(1)} %get-tuple-element.20.after_ref), channel_id=1, source_target_pairs={{8,0},{0,1},{10,2},{2,3},{12,4},{4,5},{14,6},{6,7},{16,8},{1,9},{1... | collective-permute-start | bytes 393224 | tf_op jit(solution)/shard_map/ppermute | solution.py:43
  6.5 2.2 %collective-permute-start.3 = (f32[32,8,128]{2,1,0:T(8,128)S(1)}, f32[32,8,128]{2,1,0:T(8,128)S(1)}, u32[]{:S(2)}, u32[]{:S(2)}) collective-permute-start(f32[32,8,128]{2,1,0:T(8,128)S(1)} %get-tuple-element.20.after_ref), channel_id=1, source_target_pairs={{6,0},{0,1},{8,2},{2,3},{10,4},{4,5},{12,6},{1,7},{14,8},{3,9},{16... | collective-permute-start | bytes 393224 | tf_op jit(solution)/shard_map/ppermute | solution.py:43
  8.6 1.2 %collective-permute-start.2 = (f32[32,8,128]{2,1,0:T(8,128)S(1)}, f32[32,8,128]{2,1,0:T(8,128)S(1)}, u32[]{:S(2)}, u32[]{:S(2)}) collective-permute-start(f32[32,8,128]{2,1,0:T(8,128)S(1)} %get-tuple-element.20.after_ref), channel_id=1, source_target_pairs={{4,0},{0,1},{6,2},{2,3},{8,4},{1,5},{10,6},{3,7},{12,8},{5,9},{14,... | collective-permute-start | bytes 393224 | tf_op jit(solution)/shard_map/ppermute | solution.py:43
  9.9 0.0 collective-permute-start.1
  9.9 0.0 collective-permute-done.4
  9.9 1.7 %collective-permute-done.3 = f32[32,8,128]{2,1,0:T(8,128)S(1)} collective-permute-done((f32[32,8,128]{2,1,0:T(8,128)S(1)}, f32[32,8,128]{2,1,0:T(8,128)S(1)}, u32[]{:S(2)}, u32[]{:S(2)}) %collective-permute-start.3) | collective-permute-done | bytes 131104 | tf_op jit(solution)/shard_map/ppermute | solution.py:43
  11.6 4.9 %collective-permute-done.2 = f32[32,8,128]{2,1,0:T(8,128)S(1)} collective-permute-done((f32[32,8,128]{2,1,0:T(8,128)S(1)}, f32[32,8,128]{2,1,0:T(8,128)S(1)}, u32[]{:S(2)}, u32[]{:S(2)}) %collective-permute-start.2) | collective-permute-done | bytes 131104 | tf_op jit(solution)/shard_map/ppermute | solution.py:43
  16.5 0.0 collective-permute-done.1
  16.5 0.1 collective-permute-start.5
  16.6 0.1 pad_add_fusion.refs_0_
  16.7 4.0 %spread.2.refs_6_.refs_5_ = f32[16,10,128,128]{3,2,1,0:T(8,128)S(1)} custom-call(f32[16,16,128]{2,1,0:T(8,128)S(1)} %get-tuple-element.11.rows_ref.refs_5_, f32[32,8,128]{2,1,0:T(8,128)S(1)} %get-tuple-element.20.after_ref), custom_call_target="tpu_custom_call" | custom-call | tf_op jit(solution)/shard_map/spread/pallas_call | solution.py:320
  20.6 0.0 copy-start.1
  20.6 0.0 copy-start.4
  20.7 0.0 collective-permute-done.5
  20.8 0.7 copy-done.1
  21.5 0.0 copy-done.4
  21.5 19.2 %density_sweep.1 = (f32[16,128]{1,0:T(8,128)}, f32[16,8,128]{2,1,0:T(8,128)S(1)}, f32[16,31,8,128]{3,2,1,0:T(8,128)S(1)}, s32[16,128]{1,0:T(8,128)S(1)}) custom-call(s32[2]{0:T(128)S(1)} %pad_add_fusion.refs_0_, s32[16]{0:T(128)S(1)} %copy-done.4, s32[16,128]{1,0:T(8,128)S(1)} %get-tuple-element.9.refs_2_, ...), custom_call_target="tpu_custom_call" | custom-call | tf_op jit(solution)/shard_map/density_sweep/pallas_call | solution.py:333
  40.8 0.1 collective-permute-start.6
  40.9 1.2 %collective-permute-done.6 = f32[16,8,128]{2,1,0:T(8,128)S(1)} collective-permute-done((f32[16,8,128]{2,1,0:T(8,128)S(1)}, f32[16,8,128]{2,1,0:T(8,128)S(1)}, u32[]{:S(2)}, u32[]{:S(2)}) %collective-permute-start.6) | collective-permute-done | bytes 65568 | tf_op jit(solution)/shard_map/ppermute | solution.py:22
  42.1 0.0 collective-permute-start.10
  42.1 1.6 %collective-permute-start.9 = (f32[32,8,128]{2,1,0:T(8,128)S(1)}, f32[32,8,128]{2,1,0:T(8,128)S(1)}, u32[]{:S(2)}, u32[]{:S(2)}) collective-permute-start(f32[32,8,128]{2,1,0:T(8,128)S(1)} %get-tuple-element.16.after_ref), channel_id=1, source_target_pairs={{6,0},{0,1},{8,2},{2,3},{10,4},{4,5},{12,6},{1,7},{14,8},{3,9},{16... | collective-permute-start | bytes 393224 | tf_op jit(solution)/shard_map/ppermute | solution.py:43
  43.7 0.2 collective-permute-start.8
  43.9 0.3 collective-permute-start.7
  44.2 2.1 %collective-permute-done.10 = f32[32,8,128]{2,1,0:T(8,128)S(1)} collective-permute-done((f32[32,8,128]{2,1,0:T(8,128)S(1)}, f32[32,8,128]{2,1,0:T(8,128)S(1)}, u32[]{:S(2)}, u32[]{:S(2)}) %collective-permute-start.10) | collective-permute-done | bytes 131104 | tf_op jit(solution)/shard_map/ppermute | solution.py:43
  46.2 1.0 %collective-permute-done.9 = f32[32,8,128]{2,1,0:T(8,128)S(1)} collective-permute-done((f32[32,8,128]{2,1,0:T(8,128)S(1)}, f32[32,8,128]{2,1,0:T(8,128)S(1)}, u32[]{:S(2)}, u32[]{:S(2)}) %collective-permute-start.9) | collective-permute-done | bytes 131104 | tf_op jit(solution)/shard_map/ppermute | solution.py:43
  47.2 4.5 %collective-permute-done.8 = f32[32,8,128]{2,1,0:T(8,128)S(1)} collective-permute-done((f32[32,8,128]{2,1,0:T(8,128)S(1)}, f32[32,8,128]{2,1,0:T(8,128)S(1)}, u32[]{:S(2)}, u32[]{:S(2)}) %collective-permute-start.8) | collective-permute-done | bytes 131104 | tf_op jit(solution)/shard_map/ppermute | solution.py:43
  51.7 0.0 collective-permute-done.7
  51.8 0.1 collective-permute-start.11
  51.8 2.7 %spread.3.refs_6_ = f32[16,3,128,128]{3,2,1,0:T(8,128)S(1)} custom-call(f32[16,8,128]{2,1,0:T(8,128)S(1)} %get-tuple-element.14.rows_ref, f32[32,8,128]{2,1,0:T(8,128)S(1)} %get-tuple-element.16.after_ref), custom_call_target="tpu_custom_call" | custom-call | tf_op jit(solution)/shard_map/spread/pallas_call | solution.py:320
  54.6 0.0 collective-permute-done.11
  54.7 29.8 %force_sweep.1 = f32[3,16,128]{2,1,0:T(8,128)} custom-call(s32[16]{0:T(128)S(1)} %copy-done.4, s32[16,128]{1,0:T(8,128)S(1)} %get-tuple-element.13.refs_1_, f32[288,8,128]{2,1,0:T(8,128)S(1)} %constant_dynamic-update-slice_fusion.2.refs_3_.refs_2_, f32[288,8,128]{2,1,0:T(8,128)S(1)} %constant_dynamic-update-slice_fusion.11.refs_3_, ...), custom_call_target="tpu_custom_call" | custom-call | tf_op jit(solution)/shard_map/force_sweep/pallas_call | solution.py:353
  (16 shorter events, 0.3 us)
Async XLA Ops:
  0.6 0.9 %copy-start = (f32[16,9,128]{2,0,1:T(8,128)S(1)}, f32[16,9,128]{2,0,1:T(8,128)}, u32[]{:S(2)}) copy-start(f32[16,9,128]{2,0,1:T(8,128)} %param.3) | copy-start | bytes 221188
  1.5 0.7 copy-start.2
  2.2 0.7 copy-start.3
  3.5 1.6 %collective-permute-start = (f32[16,8,128]{2,1,0:T(8,128)S(1)}, f32[16,8,128]{2,1,0:T(8,128)S(1)}, u32[]{:S(2)}, u32[]{:S(2)}) collective-permute-start(f32[16,8,128]{2,1,0:T(8,128)S(1)} %get-tuple-element.10), channel_id=1, source_target_pairs={{0,1},{1,0},{2,3},{3,2},{4,5},{5,4},{6,7},{7,6},{8,9},{9,8},{10,11... | collective-permute-start | bytes 196616 | tf_op jit(solution)/shard_map/ppermute | solution.py:22
  5.2 4.7 %collective-permute-start.4 = (f32[32,8,128]{2,1,0:T(8,128)S(1)}, f32[32,8,128]{2,1,0:T(8,128)S(1)}, u32[]{:S(2)}, u32[]{:S(2)}) collective-permute-start(f32[32,8,128]{2,1,0:T(8,128)S(1)} %get-tuple-element.20.after_ref), channel_id=1, source_target_pairs={{8,0},{0,1},{10,2},{2,3},{12,4},{4,5},{14,6},{6,7},{16,8},{1,9},{1... | collective-permute-start | bytes 393224 | tf_op jit(solution)/shard_map/ppermute | solution.py:43
  6.5 5.1 %collective-permute-start.3 = (f32[32,8,128]{2,1,0:T(8,128)S(1)}, f32[32,8,128]{2,1,0:T(8,128)S(1)}, u32[]{:S(2)}, u32[]{:S(2)}) collective-permute-start(f32[32,8,128]{2,1,0:T(8,128)S(1)} %get-tuple-element.20.after_ref), channel_id=1, source_target_pairs={{6,0},{0,1},{8,2},{2,3},{10,4},{4,5},{12,6},{1,7},{14,8},{3,9},{16... | collective-permute-start | bytes 393224 | tf_op jit(solution)/shard_map/ppermute | solution.py:43
  8.6 7.8 %collective-permute-start.2 = (f32[32,8,128]{2,1,0:T(8,128)S(1)}, f32[32,8,128]{2,1,0:T(8,128)S(1)}, u32[]{:S(2)}, u32[]{:S(2)}) collective-permute-start(f32[32,8,128]{2,1,0:T(8,128)S(1)} %get-tuple-element.20.after_ref), channel_id=1, source_target_pairs={{4,0},{0,1},{6,2},{2,3},{8,4},{1,5},{10,6},{3,7},{12,8},{5,9},{14,... | collective-permute-start | bytes 393224 | tf_op jit(solution)/shard_map/ppermute | solution.py:43
  9.9 6.6 %collective-permute-start.1 = (f32[32,8,128]{2,1,0:T(8,128)S(1)}, f32[32,8,128]{2,1,0:T(8,128)S(1)}, u32[]{:S(2)}, u32[]{:S(2)}) collective-permute-start(f32[32,8,128]{2,1,0:T(8,128)S(1)} %get-tuple-element.20.after_ref), channel_id=1, source_target_pairs={{2,0},{0,1},{4,2},{1,3},{6,4},{3,5},{8,6},{5,7},{10,8},{7,9},{12,1... | collective-permute-start | bytes 393224 | tf_op jit(solution)/shard_map/ppermute | solution.py:43
  16.5 4.2 %collective-permute-start.5 = (f32[128,8,128]{2,1,0:T(8,128)S(1)}, f32[128,8,128]{2,1,0:T(8,128)S(1)}, u32[]{:S(2)}, u32[]{:S(2)}) collective-permute-start(f32[128,8,128]{2,1,0:T(8,128)S(1)} %pad_maximum_fusion), channel_id=1, source_target_pairs={{0,1},{1,0},{2,3},{3,2},{4,5},{5,4},{6,7},{7,6},{8,9},{9,8},{10,11... | collective-permute-start | bytes 1572872 | tf_op jit(solution)/shard_map/ppermute | solution.py:22
  20.6 0.9 %copy-start.1 = (f32[16,9,128]{2,0,1:T(8,128)S(1)}, f32[16,9,128]{2,0,1:T(8,128)}, u32[]{:S(2)}) copy-start(f32[16,9,128]{2,0,1:T(8,128)} %param.3) | copy-start | bytes 221188
  20.6 0.9 %copy-start.4 = (s32[16]{0:T(128)S(1)}, s32[16]{0:T(128)}, u32[]{:S(2)}) copy-start(s32[16]{0:T(128)} %refs_0_.1) | copy-start | bytes 196
  40.8 1.3 %collective-permute-start.6 = (f32[16,8,128]{2,1,0:T(8,128)S(1)}, f32[16,8,128]{2,1,0:T(8,128)S(1)}, u32[]{:S(2)}, u32[]{:S(2)}) collective-permute-start(f32[16,8,128]{2,1,0:T(8,128)S(1)} %get-tuple-element.14.rows_ref), channel_id=1, source_target_pairs={{0,1},{1,0},{2,3},{3,2},{4,5},{5,4},{6,7},{7,6},{8,9},{9,8},{10,11... | collective-permute-start | bytes 196616 | tf_op jit(solution)/shard_map/ppermute | solution.py:22
  42.1 4.1 %collective-permute-start.10 = (f32[32,8,128]{2,1,0:T(8,128)S(1)}, f32[32,8,128]{2,1,0:T(8,128)S(1)}, u32[]{:S(2)}, u32[]{:S(2)}) collective-permute-start(f32[32,8,128]{2,1,0:T(8,128)S(1)} %get-tuple-element.16.after_ref), channel_id=1, source_target_pairs={{8,0},{0,1},{10,2},{2,3},{12,4},{4,5},{14,6},{6,7},{16,8},{1,9},{1... | collective-permute-start | bytes 393224 | tf_op jit(solution)/shard_map/ppermute | solution.py:43
  42.1 5.1 %collective-permute-start.9 = (f32[32,8,128]{2,1,0:T(8,128)S(1)}, f32[32,8,128]{2,1,0:T(8,128)S(1)}, u32[]{:S(2)}, u32[]{:S(2)}) collective-permute-start(f32[32,8,128]{2,1,0:T(8,128)S(1)} %get-tuple-element.16.after_ref), channel_id=1, source_target_pairs={{6,0},{0,1},{8,2},{2,3},{10,4},{4,5},{12,6},{1,7},{14,8},{3,9},{16... | collective-permute-start | bytes 393224 | tf_op jit(solution)/shard_map/ppermute | solution.py:43
  43.7 8.0 %collective-permute-start.8 = (f32[32,8,128]{2,1,0:T(8,128)S(1)}, f32[32,8,128]{2,1,0:T(8,128)S(1)}, u32[]{:S(2)}, u32[]{:S(2)}) collective-permute-start(f32[32,8,128]{2,1,0:T(8,128)S(1)} %get-tuple-element.16.after_ref), channel_id=1, source_target_pairs={{4,0},{0,1},{6,2},{2,3},{8,4},{1,5},{10,6},{3,7},{12,8},{5,9},{14,... | collective-permute-start | bytes 393224 | tf_op jit(solution)/shard_map/ppermute | solution.py:43
  43.9 7.8 %collective-permute-start.7 = (f32[32,8,128]{2,1,0:T(8,128)S(1)}, f32[32,8,128]{2,1,0:T(8,128)S(1)}, u32[]{:S(2)}, u32[]{:S(2)}) collective-permute-start(f32[32,8,128]{2,1,0:T(8,128)S(1)} %get-tuple-element.16.after_ref), channel_id=1, source_target_pairs={{2,0},{0,1},{4,2},{1,3},{6,4},{3,5},{8,6},{5,7},{10,8},{7,9},{12,1... | collective-permute-start | bytes 393224 | tf_op jit(solution)/shard_map/ppermute | solution.py:43
  51.8 2.8 %collective-permute-start.11 = (f32[128,8,128]{2,1,0:T(8,128)S(1)}, f32[128,8,128]{2,1,0:T(8,128)S(1)}, u32[]{:S(2)}, u32[]{:S(2)}) collective-permute-start(f32[128,8,128]{2,1,0:T(8,128)S(1)} %pad_maximum_fusion.1), channel_id=1, source_target_pairs={{0,1},{1,0},{2,3},{3,2},{4,5},{5,4},{6,7},{7,6},{8,9},{9,8},{10,11... | collective-permute-start | bytes 1572872 | tf_op jit(solution)/shard_map/ppermute | solution.py:22
where the time goes:
time: 84.7 us; the launch traced here: 84.4 us
  Pallas kernels  56.3 us (66%)
  waiting for transfers between devices  16.3 us (19%)
  starting transfers between devices  7.73 us (9%)
  local copies, waits for them, and re-layouts  3.18 us (4%)
    pallas_call x1, Pallas kernels, per_device(): pl.pallas_call(lambda *refs: force_kernel(*refs, columns=columns), out_sh...  29.8 us
    pallas_call x1, Pallas kernels, per_device(): pl.pallas_call(lambda *refs: density_kernel(*refs, columns=columns, chips...  19.2 us
    ppermute x8, waiting for transfers between devices, surround(): fetched.append(lax.ppermute(chip_block, AXES, route_of(chips, k)))  14.2 us
    ppermute x8, starting transfers between devices, surround(): fetched.append(lax.ppermute(chip_block, AXES, route_of(chips, k)))  6.77 us
    pallas_call x2, Pallas kernels, spread(): pl.pallas_call(spread_kernel, out_shape=floats(local_cells, channels, LAN...  6.63 us
    unnamed x20, local copies, waits for them, and re-layouts  3.09 us
    ppermute x4, waiting for transfers between devices, swap_cores(): return lax.ppermute(block, 'group', [(0, 1), (1, 0)])  2.12 us
  transfers between devices with their start and end apart: 12, of which 7 were waited for; matrix products, arithmetic and copies ran while one was open for 0% of the time, Pallas kernels for 8%

commit v1 on v0

--- a/solution.py
+++ b/solution.py
@@ -56,31 +56,28 @@
     return [((2 * where + half) * local_cells, where) for where, half in runs]
 
 
-def pack_sources(cell, codes_ref, columns, tables, packs, pad_tiles):
+def pack_sources(cell, local_cells, index_ref, entries, table, lift, pack, pad_tiles):
     lane = lax.broadcasted_iota(jnp.int32, (1, LANES), 1)
-    held = [jnp.zeros(pack.shape[1:], jnp.float32) for pack in packs]
-    place = jnp.int32(0)
-    for entry in range(2 * columns + 1):
-        code = codes_ref[cell, entry]
-        row = lax.shift_right_logical(code, 8)
-        count = lax.bitwise_and(code, 255)
-        tile = lax.shift_right_logical(place, 7)
-        turn = lax.bitwise_and(place, 127)
-        place = place + count
-        crossed = lax.shift_right_logical(place, 7) > tile
-        beyond = lane >= turn
-        for n, (table, pack) in enumerate(zip(tables, packs)):
-            rolled = pltpu.roll(table[row], turn, 1)
-            merged = jnp.where(beyond, rolled, held[n])
-            pack[tile] = merged
-            held[n] = jnp.where(crossed, rolled, merged)
-    tile = lax.shift_right_logical(place, 7)
-    inside = lane < lax.bitwise_and(place, 127)
-    for n, pack in enumerate(packs):
-        pack[tile] = jnp.where(inside, held[n], 0.0)
-        for extra in range(1, pad_tiles):
-            pack[tile + extra] = jnp.zeros(pack.shape[1:], jnp.float32)
-    return lax.shift_right_logical(place + 127, 7)
+    held = jnp.zeros(pack.shape[1:], jnp.float32)
+    tile = index_ref[local_cells + cell, 0]
+    for entry in range(entries):
+        turn = index_ref[2 * local_cells + cell, entry]
+        following = index_ref[local_cells + cell, entry + 1]
+        rolled = pltpu.roll(lift(table[index_ref[cell, entry]]), turn, 1)
+        merged = jnp.where(lane >= turn, rolled, held)
+        pack[tile] = merged
+        held = jnp.where(following > tile, rolled, merged)
+        tile = following
+    turn = index_ref[2 * local_cells + cell, entries]
+    pack[tile] = jnp.where(lane < turn, held, 0.0)
+    for extra in range(1, pad_tiles):
+        pack[tile + extra] = jnp.zeros(pack.shape[1:], jnp.float32)
+    return jnp.where(turn > 0, tile + 1, tile)
+
+
+def count_of(cell, local_cells, index_ref, entry):
+    tiles = index_ref[local_cells + cell, entry + 1] - index_ref[local_cells + cell, entry]
+    return 128 * tiles + index_ref[2 * local_cells + cell, entry + 1] - index_ref[2 * local_cells + cell, entry]
 
 
 def each_group(count, tile_count, body, finish, zeros):
@@ -133,7 +130,8 @@
         sent_ref[cell, 7:8, :] = ((padded_ref[row, :] + 1) * 256 + count).astype(jnp.float32)
     smooth = particles_ref[6]
     steep = slope_norm ** (1.0 / 3.0) * jnp.exp((-5.0 / 3.0) * jnp.log(smooth))
-    rows = [particles_ref[d] for d in range(6)] + [2.0 / smooth, smooth * 0.05, steep, steep * (0.5 / smooth)]
+    rows = [particles_ref[d] for d in range(6)]
+    rows += [2.0 / smooth, smooth * 0.05, steep, steep * (0.5 / smooth), smooth, particles_ref[8]]
     for cell in range(local_cells):
         for c, row in enumerate(rows):
             own_ref[cell, c : c + 1, :] = row[cell : cell + 1]
@@ -151,12 +149,13 @@
     lax.fori_loop(0, spread_ref.shape[0] // 2, per_pair, 0)
 
 
-def partner_codes(place_ref, padded_ref, table_ref, code_ref, listed_ref, found_ref, columns, chips):
+def find_partners(padded_ref, table_ref, code_ref, listed_ref, found_ref, columns):
+    chips = lax.axis_size("curve")
     local_cells = padded_ref.shape[0]
     reach = reach_of(local_cells)
     lane = lax.broadcasted_iota(jnp.int32, (1, LANES), 1)
     inner = lax.broadcasted_iota(jnp.int32, (8, LANES), 0)
-    starts = window_starts(place_ref[0], place_ref[1], local_cells, reach)
+    starts = window_starts(lax.axis_index("curve"), lax.axis_index("group"), local_cells, reach)
     groups = []
     for first in range(0, table_ref.shape[0], 8):
         start, where = starts[first // local_cells]
@@ -185,18 +184,32 @@
         return carry
 
     lax.fori_loop(0, local_cells, per_cell, 0)
+    code = found_ref[0:local_cells, :]
+    count = lax.bitwise_and(code, 255)
+    place, shift = count, 1
+    while shift < 2 * columns + 1:
+        place = place + jnp.where(lane >= shift, pltpu.roll(place, shift, 1), 0)
+        shift *= 2
+    place = place - count
+    found_ref[0:local_cells, :] = lax.shift_right_logical(code, 8)
+    found_ref[local_cells : 2 * local_cells, :] = lax.shift_right_logical(place, 7)
+    found_ref[2 * local_cells : 3 * local_cells, :] = lax.bitwise_and(place, 127)
 
 
 def density_kernel(
-    place_ref, counts_ref, padded_ref, table_ref, particles_ref, own_ref, spread_ref,
-    out_ref, state_ref, pack_ref, codes_ref, sums_ref, code_ref, listed_ref, found_ref, *, columns, chips,
+    padded_ref, table_ref, own_ref, spread_ref,
+    out_ref, sent_ref, state_ref, pack_ref, index_ref, sums_ref, code_ref, listed_ref, found_ref, *, columns,
 ):
-    local_cells = particles_ref.shape[1]
-    partner_codes(place_ref, padded_ref, table_ref, code_ref, listed_ref, found_ref, columns, chips)
-    pltpu.sync_copy(found_ref, codes_ref)
+    local_cells = out_ref.shape[0]
+    entries = 2 * columns + 1
+    find_partners(padded_ref, table_ref, code_ref, listed_ref, found_ref, columns)
+    pltpu.sync_copy(found_ref, index_ref)
 
     def per_cell(cell, carry):
-        tile_count = pack_sources(cell, codes_ref, columns, [table_ref], [pack_ref.at[cell]], 2)
+        tile_count = pack_sources(
+            cell, local_cells, index_ref, entries, table_ref, lambda held: held, pack_ref.at[cell], 2
+        )
+        count = count_of(cell, local_cells, index_ref, columns)
 
         def body(span):
             xa, ya, za, ia = (spread_ref[cell, c, span, :] for c in (0, 1, 2, 6))
@@ -219,13 +232,14 @@
         def finish(span, total):
             sums_ref[cell, span, :] = total
 
-        each_group(counts_ref[cell], tile_count, body, finish, lambda rows: jnp.zeros((rows, LANES), jnp.float32))
+        each_group(count, tile_count, body, finish, lambda rows: jnp.zeros((rows, LANES), jnp.float32))
         return carry
 
     lax.fori_loop(0, local_cells, per_cell, 0)
     raw = row_sums(sums_ref, local_cells)
     masses = jnp.concatenate([table_ref[cell, 3:4, :] for cell in range(local_cells)], axis=0)
-    smooth, entropy = particles_ref[6], particles_ref[8]
+    smooth = jnp.concatenate([own_ref[cell, 10:11, :] for cell in range(local_cells)], axis=0)
+    entropy = jnp.concatenate([own_ref[cell, 11:12, :] for cell in range(local_cells)], axis=0)
     held = masses > 0.0
     smooth = jnp.where(held, smooth, 1.0)
     density = jnp.where(held, raw * (kernel_norm / 256.0) / (smooth * smooth * smooth), 0.0)
@@ -238,18 +252,31 @@
     for cell in range(local_cells):
         for c, row in enumerate(rows):
             state_ref[cell, c : c + 1, :] = row[cell : cell + 1]
-        state_ref[cell, 3:6, :] = own_ref[cell, 7:10, :]
-        state_ref[cell, 6:8, :] = jnp.zeros((2, LANES), jnp.float32)
+        state_ref[cell, 3:8, :] = jnp.zeros((5, LANES), jnp.float32)
+        for c in range(2):
+            sent_ref[cell, c : c + 1, :] = rows[c][cell : cell + 1]
+        sent_ref[cell, 2:3, :] = own_ref[cell, 8:9, :]
+        sent_ref[cell, 3:4, :] = own_ref[cell, 7:8, :]
+
+
+def with_sound(held):
+    squared = (0.025 * 0.025 * 200.0 * gamma_index) * (held[0:1] * held[1:2])
+    sound = squared * lax.rsqrt(jnp.maximum(squared, TINY))
+    return jnp.concatenate([held, sound, 0.025 * held[2:3] / held[3:4]], axis=0)
 
 
 def force_kernel(
-    counts_ref, codes_ref, table_ref, state_ref, pack_ref, spread_ref, state_spread_ref,
+    index_ref, table_ref, state_ref, pack_ref, spread_ref, state_spread_ref,
     out_ref, state_pack_ref, sums_ref, *, columns,
 ):
     local_cells = out_ref.shape[1]
+    entries = 2 * columns + 1
 
     def per_cell(cell, carry):
-        tile_count = pack_sources(cell, codes_ref, columns, [state_ref], [state_pack_ref], 2)
+        tile_count = pack_sources(
+            cell, local_cells, index_ref, entries, state_ref, with_sound, state_pack_ref, 2
+        )
+        count = count_of(cell, local_cells, index_ref, columns)
 
         def body(span):
             def step(first, tiles, total):
@@ -259,7 +286,7 @@
                     ga, sa, ja = (spread_ref[cell, c, span, :] for c in range(7, 10))
                     ra, fa, ca = (state_spread_ref[cell, c, span, :] for c in range(3))
                     xb, yb, zb, mb, ub, vb, wb = (pack_ref[cell, at, c : c + 1, :] for c in range(7))
-                    rb, fb, cb, gb, sb, jb = (state_pack_ref[at, c : c + 1, :] for c in range(6))
+                    rb, fb, sb, gb, cb, jb = (state_pack_ref[at, c : c + 1, :] for c in range(6))
                     dx, dy, dz = xa - xb, ya - yb, za - zb
                     squared = dx * dx + dy * dy + dz * dz
                     apart = squared * lax.rsqrt(jnp.maximum(squared, TINY))
@@ -282,7 +309,7 @@
                 sums_ref[d, cell, span, :] = total[d]
 
         each_group(
-            counts_ref[cell], tile_count, body, finish, lambda rows: (jnp.zeros((rows, LANES), jnp.float32),) * 3
+            count, tile_count, body, finish, lambda rows: (jnp.zeros((rows, LANES), jnp.float32),) * 3
         )
         return carry
 
@@ -294,6 +321,10 @@
 
 def on_chip(array):
     return pltpu.with_memory_space_constraint(array, pltpu.VMEM)
+
+
+def off_chip(array):
+    return pltpu.with_memory_space_constraint(array, pltpu.HBM)
 
 
 def per_device(particles, counts, pair_lists):
@@ -304,8 +335,6 @@
     whole = pl.BlockSpec(memory_space=pltpu.VMEM)
     plain = lambda *shape: jax.ShapeDtypeStruct(shape, jnp.float32)
     floats = lambda *shape: pltpu.VMEM(shape, jnp.float32)
-    chips = lax.axis_size("curve")
-    place = jnp.stack([lax.axis_index("curve"), lax.axis_index("group")]).astype(jnp.int32)
     particles = jnp.transpose(particles, (1, 0, 2))
     sent, padded, own = pl.pallas_call(
         prepare_kernel,
@@ -314,7 +343,7 @@
         out_specs=(whole, whole, whole),
         name="prepare",
         compiler_params=pltpu.CompilerParams(vmem_limit_bytes=ROOM),
-    )(counts, particles, pair_lists)
+    )(counts, off_chip(particles), off_chip(pair_lists))
 
     def spread(rows, channels, after):
         return pl.pallas_call(
@@ -330,35 +359,36 @@
     table = on_chip(window)
     most_tiles = 2 * columns + 5
     rows = table.shape[0]
-    density, state, packed, codes = pl.pallas_call(
-        lambda *refs: density_kernel(*refs, columns=columns, chips=chips),
+    density, thermal, state, packed, index = pl.pallas_call(
+        lambda *refs: density_kernel(*refs, columns=columns),
         out_shape=(
             plain(local_cells, slots),
-            plain(local_cells, 8, slots),
+            plain(local_cells, 4, slots),
+            floats(local_cells, 8, slots),
             floats(local_cells, most_tiles, 8, LANES),
-            jax.ShapeDtypeStruct((local_cells, LANES), jnp.int32),
+            jax.ShapeDtypeStruct((3 * local_cells, LANES), jnp.int32),
         ),
-        in_specs=[scalars, scalars, whole, whole, whole, whole, whole],
-        out_specs=(whole, whole, whole, scalars),
+        in_specs=[whole, whole, whole, whole],
+        out_specs=(whole, whole, whole, whole, scalars),
         scratch_shapes=[
             floats(local_cells, LANES, LANES),
             floats(rows, LANES),
             floats(rows, LANES),
-            pltpu.VMEM((local_cells, LANES), jnp.int32),
+            pltpu.VMEM((3 * local_cells, LANES), jnp.int32),
         ],
         name="density_sweep",
         compiler_params=pltpu.CompilerParams(vmem_limit_bytes=ROOM),
-    )(place, counts, padded, table, particles, own, own_spread)
-    states, state_spread = surround(state, lambda after: spread(state, 3, after))
+    )(padded, table, own, own_spread)
+    states, state_spread = surround(thermal, lambda after: spread(state, 3, after))
     acceleration = pl.pallas_call(
         lambda *refs: force_kernel(*refs, columns=columns),
         out_shape=plain(3, local_cells, slots),
-        in_specs=[scalars, scalars, whole, whole, whole, whole, whole],
+        in_specs=[scalars, whole, whole, whole, whole, whole],
         out_specs=whole,
-        scratch_shapes=[floats(most_tiles, 8, LANES), floats(3, local_cells, LANES, LANES)],
+        scratch_shapes=[floats(most_tiles, 6, LANES), floats(3, local_cells, LANES, LANES)],
         name="force_sweep",
         compiler_params=pltpu.CompilerParams(vmem_limit_bytes=ROOM),
-    )(counts, codes, table, on_chip(states), packed, own_spread, state_spread)
+    )(index, table, on_chip(states), packed, own_spread, state_spread)
     return density, jnp.transpose(acceleration, (1, 0, 2))
 
 

time: 84.7 us -> 77.5 us (0.915)
  waiting for transfers between devices: 16.3 us -> 12.2 us
  local copies, waits for them, and re-layouts: 3.18 us -> 0.87 us
    ppermute x8, waiting for transfers between devices: 14.2 us -> 8.66 us  [surround(): fetched.append(lax.ppermute(chip_block, AXES, route_of(chips, k)))]
    unnamed x20 -> x12, local copies, waits for them, and re-layouts: 3.09 us -> 0.77 us
    ppermute x4, waiting for transfers between devices: 2.12 us -> 3.51 us  [swap_cores(): return lax.ppermute(block, 'group', [(0, 1), (1, 0)])]
  transfers between devices with their start and end apart: 12 -> 12, of which waited for: 7 -> 6; matrix products, arithmetic and copies ran while one was open for 0% -> 0% of each run, Pallas kernels for 8% -> 9%
where the time goes in v1:
time: 77.5 us; the launch traced here: 77.4 us
  Pallas kernels  55.6 us (72%)
  waiting for transfers between devices  12.2 us (16%)
  starting transfers between devices  7.79 us (10%)
  local copies, waits for them, and re-layouts  0.87 us (1%)
  between operations  0.81 us (1%)
    pallas_call x1, Pallas kernels, per_device(): pl.pallas_call(lambda *refs: force_kernel(*refs, columns=columns), out_sh...  29.6 us
    pallas_call x1, Pallas kernels, per_device(): pl.pallas_call(lambda *refs: density_kernel(*refs, columns=columns), out_...  18.5 us
    ppermute x8, waiting for transfers between devices, surround(): fetched.append(lax.ppermute(chip_block, AXES, route_of(chips, k)))  8.66 us
    ppermute x8, starting transfers between devices, surround(): fetched.append(lax.ppermute(chip_block, AXES, route_of(chips, k)))  6.83 us
    pallas_call x2, Pallas kernels, spread(): pl.pallas_call(spread_kernel, out_shape=floats(local_cells, channels, LAN...  6.63 us
    ppermute x4, waiting for transfers between devices, swap_cores(): return lax.ppermute(block, 'group', [(0, 1), (1, 0)])  3.51 us
  transfers between devices with their start and end apart: 12, of which 6 were waited for; matrix products, arithmetic and copies ran while one was open for 0% of the time, Pallas kernels for 9%

profile of v1, /device:TPU:13, one launch (start us, length us, event | category | flops | bytes accessed | tf_op | source)
XLA Modules:
  0.0 77.4 jit_solution(3394228718144423875)
XLA Ops:
  0.6 0.0 copy-start
  0.6 0.6 copy-done
  1.3 1.0 %prepare.1 = (f32[16,8,128]{2,1,0:T(8,128)S(1)}, s32[16,128]{1,0:T(8,128)S(1)}, f32[16,16,128]{2,1,0:T(8,128)S(1)}) custom-call(s32[16]{0:T(128)S(1)} %copy-done, f32[9,16,128]{2,1,0:T(8,128)} %bitcast.2, s32[16,13]{1,0:T(8,128)} %lists_ref.1), custom_call_target="tpu_custom_call" | custom-call | tf_op jit(solution)/shard_map/prepare/pallas_call | solution.py:339
  2.3 0.7 collective-permute-start
  3.0 0.9 %collective-permute-done = f32[16,8,128]{2,1,0:T(8,128)S(1)} collective-permute-done((f32[16,8,128]{2,1,0:T(8,128)S(1)}, f32[16,8,128]{2,1,0:T(8,128)S(1)}, u32[]{:S(2)}, u32[]{:S(2)}) %collective-permute-start) | collective-permute-done | bytes 65568 | tf_op jit(solution)/shard_map/ppermute | solution.py:22
  3.9 1.3 %collective-permute-start.4 = (f32[32,8,128]{2,1,0:T(8,128)S(1)}, f32[32,8,128]{2,1,0:T(8,128)S(1)}, u32[]{:S(2)}, u32[]{:S(2)}) collective-permute-start(f32[32,8,128]{2,1,0:T(8,128)S(1)} %get-tuple-element.18.after_ref), channel_id=1, source_target_pairs={{8,0},{0,1},{10,2},{2,3},{12,4},{4,5},{14,6},{6,7},{16,8},{1,9},{1... | collective-permute-start | bytes 393224 | tf_op jit(solution)/shard_map/ppermute | solution.py:43
  5.2 2.2 %collective-permute-start.3 = (f32[32,8,128]{2,1,0:T(8,128)S(1)}, f32[32,8,128]{2,1,0:T(8,128)S(1)}, u32[]{:S(2)}, u32[]{:S(2)}) collective-permute-start(f32[32,8,128]{2,1,0:T(8,128)S(1)} %get-tuple-element.18.after_ref), channel_id=1, source_target_pairs={{6,0},{0,1},{8,2},{2,3},{10,4},{4,5},{12,6},{1,7},{14,8},{3,9},{16... | collective-permute-start | bytes 393224 | tf_op jit(solution)/shard_map/ppermute | solution.py:43
  7.4 1.2 %collective-permute-start.2 = (f32[32,8,128]{2,1,0:T(8,128)S(1)}, f32[32,8,128]{2,1,0:T(8,128)S(1)}, u32[]{:S(2)}, u32[]{:S(2)}) collective-permute-start(f32[32,8,128]{2,1,0:T(8,128)S(1)} %get-tuple-element.18.after_ref), channel_id=1, source_target_pairs={{4,0},{0,1},{6,2},{2,3},{8,4},{1,5},{10,6},{3,7},{12,8},{5,9},{14,... | collective-permute-start | bytes 393224 | tf_op jit(solution)/shard_map/ppermute | solution.py:43
  8.7 0.0 collective-permute-start.1
  8.7 0.0 collective-permute-done.4
  8.7 1.7 %collective-permute-done.3 = f32[32,8,128]{2,1,0:T(8,128)S(1)} collective-permute-done((f32[32,8,128]{2,1,0:T(8,128)S(1)}, f32[32,8,128]{2,1,0:T(8,128)S(1)}, u32[]{:S(2)}, u32[]{:S(2)}) %collective-permute-start.3) | collective-permute-done | bytes 131104 | tf_op jit(solution)/shard_map/ppermute | solution.py:43
  10.4 4.9 %collective-permute-done.2 = f32[32,8,128]{2,1,0:T(8,128)S(1)} collective-permute-done((f32[32,8,128]{2,1,0:T(8,128)S(1)}, f32[32,8,128]{2,1,0:T(8,128)S(1)}, u32[]{:S(2)}, u32[]{:S(2)}) %collective-permute-start.2) | collective-permute-done | bytes 131104 | tf_op jit(solution)/shard_map/ppermute | solution.py:43
  15.3 0.0 collective-permute-done.1
  15.3 0.1 collective-permute-start.5
  15.4 4.0 %spread.2.refs_3_.refs_4_ = f32[16,10,128,128]{3,2,1,0:T(8,128)S(1)} custom-call(f32[16,16,128]{2,1,0:T(8,128)S(1)} %get-tuple-element.12.rows_ref.refs_2_, f32[32,8,128]{2,1,0:T(8,128)S(1)} %get-tuple-element.18.after_ref), custom_call_target="tpu_custom_call" | custom-call | tf_op jit(solution)/shard_map/spread/pallas_call | solution.py:349
  19.4 0.0 collective-permute-done.5
  19.5 18.5 %density_sweep.1 = (f32[16,128]{1,0:T(8,128)}, f32[16,4,128]{2,1,0:T(4,128)S(1)}, f32[16,8,128]{2,1,0:T(8,128)S(1)}, f32[16,31,8,128]{3,2,1,0:T(8,128)S(1)}, s32[48,128]{1,0:T(8,128)S(1)}) custom-call(s32[16,128]{1,0:T(8,128)S(1)} %get-tuple-element.10.refs_0_, f32[288,8,128]{2,1,0:T(8,128)S(1)} %constant_dynamic-update-slice_fusion.2.refs_1_, ...), custom_call_target="tpu_custom_call" | custom-call | tf_op jit(solution)/shard_map/density_sweep/pallas_call | solution.py:362
  37.9 0.1 collective-permute-start.6
  38.0 1.2 %collective-permute-done.6 = f32[16,4,128]{2,1,0:T(4,128)S(1)} collective-permute-done((f32[16,4,128]{2,1,0:T(4,128)S(1)}, f32[16,4,128]{2,1,0:T(4,128)S(1)}, u32[]{:S(2)}, u32[]{:S(2)}) %collective-permute-start.6) | collective-permute-done | bytes 32800 | tf_op jit(solution)/shard_map/ppermute | solution.py:22
  39.2 0.0 collective-permute-start.10
  39.3 1.6 %collective-permute-start.9 = (f32[32,4,128]{2,1,0:T(4,128)S(1)}, f32[32,4,128]{2,1,0:T(4,128)S(1)}, u32[]{:S(2)}, u32[]{:S(2)}) collective-permute-start(f32[32,4,128]{2,1,0:T(4,128)S(1)} %get-tuple-element.22.after_ref), channel_id=1, source_target_pairs={{6,0},{0,1},{8,2},{2,3},{10,4},{4,5},{12,6},{1,7},{14,8},{3,9},{16... | collective-permute-start | bytes 196616 | tf_op jit(solution)/shard_map/ppermute | solution.py:43
  40.9 0.2 collective-permute-start.8
  41.1 0.3 collective-permute-start.7
  41.4 2.7 %spread.3.refs_5_ = f32[16,3,128,128]{3,2,1,0:T(8,128)S(1)} custom-call(f32[16,8,128]{2,1,0:T(8,128)S(1)} %get-tuple-element.17.rows_ref, f32[32,4,128]{2,1,0:T(4,128)S(1)} %get-tuple-element.22.after_ref), custom_call_target="tpu_custom_call" | custom-call | tf_op jit(solution)/shard_map/spread/pallas_call | solution.py:349
  44.0 0.0 collective-permute-done.10
  44.0 0.0 collective-permute-done.9
  44.0 2.0 %collective-permute-done.8 = f32[32,4,128]{2,1,0:T(4,128)S(1)} collective-permute-done((f32[32,4,128]{2,1,0:T(4,128)S(1)}, f32[32,4,128]{2,1,0:T(4,128)S(1)}, u32[]{:S(2)}, u32[]{:S(2)}) %collective-permute-start.8) | collective-permute-done | bytes 65568 | tf_op jit(solution)/shard_map/ppermute | solution.py:43
  46.1 0.0 collective-permute-done.7
  46.1 0.1 pad_maximum_fusion.1
  46.2 0.1 collective-permute-start.11
  46.3 1.4 %collective-permute-done.11 = f32[128,4,128]{2,1,0:T(4,128)S(1)} collective-permute-done((f32[128,4,128]{2,1,0:T(4,128)S(1)}, f32[128,4,128]{2,1,0:T(4,128)S(1)}, u32[]{:S(2)}, u32[]{:S(2)}) %collective-permute-start.11) | collective-permute-done | bytes 262176 | tf_op jit(solution)/shard_map/ppermute | solution.py:22
  47.8 29.6 %force_sweep.1 = f32[3,16,128]{2,1,0:T(8,128)} custom-call(s32[48,128]{1,0:T(8,128)S(1)} %get-tuple-element.14.refs_0_, f32[288,8,128]{2,1,0:T(8,128)S(1)} %constant_dynamic-update-slice_fusion.2.refs_1_, f32[288,4,128]{2,1,0:T(4,128)S(1)} %constant_dynamic-update-slice_fusion.11.refs_2_, f32[16,31,8,128]{3,2,1,0:T(8,128)S(1)} %get-tuple-element.16.refs_3_, ...), custom_call_target="tpu_custom_call" | custom-call | tf_op jit(solution)/shard_map/force_sweep/pallas_call | solution.py:383
  (15 shorter events, 0.3 us)
Async XLA Ops:
  0.6 0.7 copy-start
  2.3 1.6 %collective-permute-start = (f32[16,8,128]{2,1,0:T(8,128)S(1)}, f32[16,8,128]{2,1,0:T(8,128)S(1)}, u32[]{:S(2)}, u32[]{:S(2)}) collective-permute-start(f32[16,8,128]{2,1,0:T(8,128)S(1)} %get-tuple-element.11), channel_id=1, source_target_pairs={{0,1},{1,0},{2,3},{3,2},{4,5},{5,4},{6,7},{7,6},{8,9},{9,8},{10,11... | collective-permute-start | bytes 196616 | tf_op jit(solution)/shard_map/ppermute | solution.py:22
  3.9 4.7 %collective-permute-start.4 = (f32[32,8,128]{2,1,0:T(8,128)S(1)}, f32[32,8,128]{2,1,0:T(8,128)S(1)}, u32[]{:S(2)}, u32[]{:S(2)}) collective-permute-start(f32[32,8,128]{2,1,0:T(8,128)S(1)} %get-tuple-element.18.after_ref), channel_id=1, source_target_pairs={{8,0},{0,1},{10,2},{2,3},{12,4},{4,5},{14,6},{6,7},{16,8},{1,9},{1... | collective-permute-start | bytes 393224 | tf_op jit(solution)/shard_map/ppermute | solution.py:43
  5.2 5.1 %collective-permute-start.3 = (f32[32,8,128]{2,1,0:T(8,128)S(1)}, f32[32,8,128]{2,1,0:T(8,128)S(1)}, u32[]{:S(2)}, u32[]{:S(2)}) collective-permute-start(f32[32,8,128]{2,1,0:T(8,128)S(1)} %get-tuple-element.18.after_ref), channel_id=1, source_target_pairs={{6,0},{0,1},{8,2},{2,3},{10,4},{4,5},{12,6},{1,7},{14,8},{3,9},{16... | collective-permute-start | bytes 393224 | tf_op jit(solution)/shard_map/ppermute | solution.py:43
  7.4 7.8 %collective-permute-start.2 = (f32[32,8,128]{2,1,0:T(8,128)S(1)}, f32[32,8,128]{2,1,0:T(8,128)S(1)}, u32[]{:S(2)}, u32[]{:S(2)}) collective-permute-start(f32[32,8,128]{2,1,0:T(8,128)S(1)} %get-tuple-element.18.after_ref), channel_id=1, source_target_pairs={{4,0},{0,1},{6,2},{2,3},{8,4},{1,5},{10,6},{3,7},{12,8},{5,9},{14,... | collective-permute-start | bytes 393224 | tf_op jit(solution)/shard_map/ppermute | solution.py:43
  8.7 6.6 %collective-permute-start.1 = (f32[32,8,128]{2,1,0:T(8,128)S(1)}, f32[32,8,128]{2,1,0:T(8,128)S(1)}, u32[]{:S(2)}, u32[]{:S(2)}) collective-permute-start(f32[32,8,128]{2,1,0:T(8,128)S(1)} %get-tuple-element.18.after_ref), channel_id=1, source_target_pairs={{2,0},{0,1},{4,2},{1,3},{6,4},{3,5},{8,6},{5,7},{10,8},{7,9},{12,1... | collective-permute-start | bytes 393224 | tf_op jit(solution)/shard_map/ppermute | solution.py:43
  15.3 4.1 %collective-permute-start.5 = (f32[128,8,128]{2,1,0:T(8,128)S(1)}, f32[128,8,128]{2,1,0:T(8,128)S(1)}, u32[]{:S(2)}, u32[]{:S(2)}) collective-permute-start(f32[128,8,128]{2,1,0:T(8,128)S(1)} %pad_maximum_fusion), channel_id=1, source_target_pairs={{0,1},{1,0},{2,3},{3,2},{4,5},{5,4},{6,7},{7,6},{8,9},{9,8},{10,11... | collective-permute-start | bytes 1572872 | tf_op jit(solution)/shard_map/ppermute | solution.py:22
  37.9 1.3 %collective-permute-start.6 = (f32[16,4,128]{2,1,0:T(4,128)S(1)}, f32[16,4,128]{2,1,0:T(4,128)S(1)}, u32[]{:S(2)}, u32[]{:S(2)}) collective-permute-start(f32[16,4,128]{2,1,0:T(4,128)S(1)} %get-tuple-element.15), channel_id=1, source_target_pairs={{0,1},{1,0},{2,3},{3,2},{4,5},{5,4},{6,7},{7,6},{8,9},{9,8},{10,11... | collective-permute-start | bytes 98312 | tf_op jit(solution)/shard_map/ppermute | solution.py:22
  39.2 4.8 %collective-permute-start.10 = (f32[32,4,128]{2,1,0:T(4,128)S(1)}, f32[32,4,128]{2,1,0:T(4,128)S(1)}, u32[]{:S(2)}, u32[]{:S(2)}) collective-permute-start(f32[32,4,128]{2,1,0:T(4,128)S(1)} %get-tuple-element.22.after_ref), channel_id=1, source_target_pairs={{8,0},{0,1},{10,2},{2,3},{12,4},{4,5},{14,6},{6,7},{16,8},{1,9},{1... | collective-permute-start | bytes 196616 | tf_op jit(solution)/shard_map/ppermute | solution.py:43
  39.3 4.8 %collective-permute-start.9 = (f32[32,4,128]{2,1,0:T(4,128)S(1)}, f32[32,4,128]{2,1,0:T(4,128)S(1)}, u32[]{:S(2)}, u32[]{:S(2)}) collective-permute-start(f32[32,4,128]{2,1,0:T(4,128)S(1)} %get-tuple-element.22.after_ref), channel_id=1, source_target_pairs={{6,0},{0,1},{8,2},{2,3},{10,4},{4,5},{12,6},{1,7},{14,8},{3,9},{16... | collective-permute-start | bytes 196616 | tf_op jit(solution)/shard_map/ppermute | solution.py:43
  40.9 5.2 %collective-permute-start.8 = (f32[32,4,128]{2,1,0:T(4,128)S(1)}, f32[32,4,128]{2,1,0:T(4,128)S(1)}, u32[]{:S(2)}, u32[]{:S(2)}) collective-permute-start(f32[32,4,128]{2,1,0:T(4,128)S(1)} %get-tuple-element.22.after_ref), channel_id=1, source_target_pairs={{4,0},{0,1},{6,2},{2,3},{8,4},{1,5},{10,6},{3,7},{12,8},{5,9},{14,... | collective-permute-start | bytes 196616 | tf_op jit(solution)/shard_map/ppermute | solution.py:43
  41.1 5.0 %collective-permute-start.7 = (f32[32,4,128]{2,1,0:T(4,128)S(1)}, f32[32,4,128]{2,1,0:T(4,128)S(1)}, u32[]{:S(2)}, u32[]{:S(2)}) collective-permute-start(f32[32,4,128]{2,1,0:T(4,128)S(1)} %get-tuple-element.22.after_ref), channel_id=1, source_target_pairs={{2,0},{0,1},{4,2},{1,3},{6,4},{3,5},{8,6},{5,7},{10,8},{7,9},{12,1... | collective-permute-start | bytes 196616 | tf_op jit(solution)/shard_map/ppermute | solution.py:43
  46.2 1.6 %collective-permute-start.11 = (f32[128,4,128]{2,1,0:T(4,128)S(1)}, f32[128,4,128]{2,1,0:T(4,128)S(1)}, u32[]{:S(2)}, u32[]{:S(2)}) collective-permute-start(f32[128,4,128]{2,1,0:T(4,128)S(1)} %pad_maximum_fusion.1), channel_id=1, source_target_pairs={{0,1},{1,0},{2,3},{3,2},{4,5},{5,4},{6,7},{7,6},{8,9},{9,8},{10,11... | collective-permute-start | bytes 786440 | tf_op jit(solution)/shard_map/ppermute | solution.py:22

commit v2 on v1

--- a/solution.py
+++ b/solution.py
@@ -92,19 +92,20 @@
         total = lax.fori_loop(0, twos, lambda k, t: step(4 * fours, 2, t), total)
         finish(span, total)
 
-    def whole(group, carry):
-        per_group(group * 16, 16)
-        return carry
-
+    start = jnp.int32(0)
     eights = lax.shift_right_logical(count + 7, 3)
-    wholes = lax.shift_right_logical(eights, 1)
-    lax.fori_loop(0, wholes, whole, 0)
-
-    def rest(_, carry):
-        per_group(wholes * 16, 8)
-        return carry
-
-    lax.fori_loop(0, lax.bitwise_and(eights, 1), rest, 0)
+    for rows, groups in (
+        (32, lax.shift_right_logical(eights, 2)),
+        (16, lax.bitwise_and(lax.shift_right_logical(eights, 1), 1)),
+        (8, lax.bitwise_and(eights, 1)),
+    ):
+
+        def several(group, carry, start=start, rows=rows):
+            per_group(start + group * rows, rows)
+            return carry
+
+        lax.fori_loop(0, groups, several, 0)
+        start = start + groups * rows
 
 
 def row_sums(sums, local_cells):

time: 77.5 us -> 71.9 us (0.928)
  Pallas kernels: 55.6 us -> 49.4 us
    pallas_call x1, Pallas kernels: 29.6 us -> 25.8 us  [per_device(): pl.pallas_call(lambda *refs: force_kernel(*refs, columns=columns), out_sh...]
    pallas_call x1, Pallas kernels: 18.5 us -> 16 us  [per_device(): pl.pallas_call(lambda *refs: density_kernel(*refs, columns=columns), out_...]
where the time goes in v2:
time: 71.9 us; the launch traced here: 71.7 us
  Pallas kernels  49.4 us (69%)
  waiting for transfers between devices  12.3 us (17%)
  starting transfers between devices  8.17 us (11%)
  local copies, waits for them, and re-layouts  0.87 us (1%)
  between operations  0.8 us (1%)
    pallas_call x1, Pallas kernels, per_device(): pl.pallas_call(lambda *refs: force_kernel(*refs, columns=columns), out_sh...  25.8 us
    pallas_call x1, Pallas kernels, per_device(): pl.pallas_call(lambda *refs: density_kernel(*refs, columns=columns), out_...  16 us
    ppermute x8, waiting for transfers between devices, surround(): fetched.append(lax.ppermute(chip_block, AXES, route_of(chips, k)))  8.85 us
    ppermute x8, starting transfers between devices, surround(): fetched.append(lax.ppermute(chip_block, AXES, route_of(chips, k)))  7.18 us
    pallas_call x2, Pallas kernels, spread(): pl.pallas_call(spread_kernel, out_shape=floats(local_cells, channels, LAN...  6.63 us
    ppermute x4, waiting for transfers between devices, swap_cores(): return lax.ppermute(block, 'group', [(0, 1), (1, 0)])  3.49 us
  transfers between devices with their start and end apart: 12, of which 6 were waited for; matrix products, arithmetic and copies ran while one was open for 0% of the time, Pallas kernels for 9%

profile of v2, /device:TPU:13, one launch (start us, length us, event | category | flops | bytes accessed | tf_op | source)
XLA Modules:
  0.0 71.7 jit_solution(6704693462486395242)
XLA Ops:
  0.6 0.0 copy-start
  0.6 0.6 copy-done
  1.3 1.0 %prepare.1 = (f32[16,8,128]{2,1,0:T(8,128)S(1)}, s32[16,128]{1,0:T(8,128)S(1)}, f32[16,16,128]{2,1,0:T(8,128)S(1)}) custom-call(s32[16]{0:T(128)S(1)} %copy-done, f32[9,16,128]{2,1,0:T(8,128)} %bitcast.2, s32[16,13]{1,0:T(8,128)} %lists_ref.1), custom_call_target="tpu_custom_call" | custom-call | tf_op jit(solution)/shard_map/prepare/pallas_call | solution.py:340
  2.3 0.7 %collective-permute-start = (f32[16,8,128]{2,1,0:T(8,128)S(1)}, f32[16,8,128]{2,1,0:T(8,128)S(1)}, u32[]{:S(2)}, u32[]{:S(2)}) collective-permute-start(f32[16,8,128]{2,1,0:T(8,128)S(1)} %get-tuple-element.11), channel_id=1, source_target_pairs={{0,1},{1,0},{2,3},{3,2},{4,5},{5,4},{6,7},{7,6},{8,9},{9,8},{10,11... | collective-permute-start | bytes 196616 | tf_op jit(solution)/shard_map/ppermute | solution.py:22
  3.0 0.9 %collective-permute-done = f32[16,8,128]{2,1,0:T(8,128)S(1)} collective-permute-done((f32[16,8,128]{2,1,0:T(8,128)S(1)}, f32[16,8,128]{2,1,0:T(8,128)S(1)}, u32[]{:S(2)}, u32[]{:S(2)}) %collective-permute-start) | collective-permute-done | bytes 65568 | tf_op jit(solution)/shard_map/ppermute | solution.py:22
  3.9 1.3 %collective-permute-start.4 = (f32[32,8,128]{2,1,0:T(8,128)S(1)}, f32[32,8,128]{2,1,0:T(8,128)S(1)}, u32[]{:S(2)}, u32[]{:S(2)}) collective-permute-start(f32[32,8,128]{2,1,0:T(8,128)S(1)} %get-tuple-element.18.after_ref), channel_id=1, source_target_pairs={{8,0},{0,1},{10,2},{2,3},{12,4},{4,5},{14,6},{6,7},{16,8},{1,9},{1... | collective-permute-start | bytes 393224 | tf_op jit(solution)/shard_map/ppermute | solution.py:43
  5.2 2.2 %collective-permute-start.3 = (f32[32,8,128]{2,1,0:T(8,128)S(1)}, f32[32,8,128]{2,1,0:T(8,128)S(1)}, u32[]{:S(2)}, u32[]{:S(2)}) collective-permute-start(f32[32,8,128]{2,1,0:T(8,128)S(1)} %get-tuple-element.18.after_ref), channel_id=1, source_target_pairs={{6,0},{0,1},{8,2},{2,3},{10,4},{4,5},{12,6},{1,7},{14,8},{3,9},{16... | collective-permute-start | bytes 393224 | tf_op jit(solution)/shard_map/ppermute | solution.py:43
  7.4 1.2 %collective-permute-start.2 = (f32[32,8,128]{2,1,0:T(8,128)S(1)}, f32[32,8,128]{2,1,0:T(8,128)S(1)}, u32[]{:S(2)}, u32[]{:S(2)}) collective-permute-start(f32[32,8,128]{2,1,0:T(8,128)S(1)} %get-tuple-element.18.after_ref), channel_id=1, source_target_pairs={{4,0},{0,1},{6,2},{2,3},{8,4},{1,5},{10,6},{3,7},{12,8},{5,9},{14,... | collective-permute-start | bytes 393224 | tf_op jit(solution)/shard_map/ppermute | solution.py:43
  8.7 0.0 collective-permute-start.1
  8.7 0.0 collective-permute-done.4
  8.7 1.7 %collective-permute-done.3 = f32[32,8,128]{2,1,0:T(8,128)S(1)} collective-permute-done((f32[32,8,128]{2,1,0:T(8,128)S(1)}, f32[32,8,128]{2,1,0:T(8,128)S(1)}, u32[]{:S(2)}, u32[]{:S(2)}) %collective-permute-start.3) | collective-permute-done | bytes 131104 | tf_op jit(solution)/shard_map/ppermute | solution.py:43
  10.4 4.9 %collective-permute-done.2 = f32[32,8,128]{2,1,0:T(8,128)S(1)} collective-permute-done((f32[32,8,128]{2,1,0:T(8,128)S(1)}, f32[32,8,128]{2,1,0:T(8,128)S(1)}, u32[]{:S(2)}, u32[]{:S(2)}) %collective-permute-start.2) | collective-permute-done | bytes 131104 | tf_op jit(solution)/shard_map/ppermute | solution.py:43
  15.3 0.0 collective-permute-done.1
  15.3 0.1 collective-permute-start.5
  15.4 4.0 %spread.2.refs_3_.refs_4_ = f32[16,10,128,128]{3,2,1,0:T(8,128)S(1)} custom-call(f32[16,16,128]{2,1,0:T(8,128)S(1)} %get-tuple-element.12.rows_ref.refs_2_, f32[32,8,128]{2,1,0:T(8,128)S(1)} %get-tuple-element.18.after_ref), custom_call_target="tpu_custom_call" | custom-call | tf_op jit(solution)/shard_map/spread/pallas_call | solution.py:350
  19.4 0.0 collective-permute-done.5
  19.5 16.0 %density_sweep.1 = (f32[16,128]{1,0:T(8,128)}, f32[16,4,128]{2,1,0:T(4,128)S(1)}, f32[16,8,128]{2,1,0:T(8,128)S(1)}, f32[16,31,8,128]{3,2,1,0:T(8,128)S(1)}, s32[48,128]{1,0:T(8,128)S(1)}) custom-call(s32[16,128]{1,0:T(8,128)S(1)} %get-tuple-element.10.refs_0_, f32[288,8,128]{2,1,0:T(8,128)S(1)} %constant_dynamic-update-slice_fusion.2.refs_1_, ...), custom_call_target="tpu_custom_call" | custom-call | tf_op jit(solution)/shard_map/density_sweep/pallas_call | solution.py:363
  35.5 0.1 collective-permute-start.6
  35.6 1.2 %collective-permute-done.6 = f32[16,4,128]{2,1,0:T(4,128)S(1)} collective-permute-done((f32[16,4,128]{2,1,0:T(4,128)S(1)}, f32[16,4,128]{2,1,0:T(4,128)S(1)}, u32[]{:S(2)}, u32[]{:S(2)}) %collective-permute-start.6) | collective-permute-done | bytes 32800 | tf_op jit(solution)/shard_map/ppermute | solution.py:22
  36.8 0.0 collective-permute-start.10
  36.8 2.2 %collective-permute-start.9 = (f32[32,4,128]{2,1,0:T(4,128)S(1)}, f32[32,4,128]{2,1,0:T(4,128)S(1)}, u32[]{:S(2)}, u32[]{:S(2)}) collective-permute-start(f32[32,4,128]{2,1,0:T(4,128)S(1)} %get-tuple-element.22.after_ref), channel_id=1, source_target_pairs={{6,0},{0,1},{8,2},{2,3},{10,4},{4,5},{12,6},{1,7},{14,8},{3,9},{16... | collective-permute-start | bytes 196616 | tf_op jit(solution)/shard_map/ppermute | solution.py:43
  39.0 0.0 collective-permute-start.8
  39.0 0.3 collective-permute-start.7
  39.2 2.7 %spread.3.refs_5_ = f32[16,3,128,128]{3,2,1,0:T(8,128)S(1)} custom-call(f32[16,8,128]{2,1,0:T(8,128)S(1)} %get-tuple-element.17.rows_ref, f32[32,4,128]{2,1,0:T(4,128)S(1)} %get-tuple-element.22.after_ref), custom_call_target="tpu_custom_call" | custom-call | tf_op jit(solution)/shard_map/spread/pallas_call | solution.py:350
  41.9 0.0 collective-permute-done.10
  41.9 0.0 collective-permute-done.9
  41.9 2.2 %collective-permute-done.8 = f32[32,4,128]{2,1,0:T(4,128)S(1)} collective-permute-done((f32[32,4,128]{2,1,0:T(4,128)S(1)}, f32[32,4,128]{2,1,0:T(4,128)S(1)}, u32[]{:S(2)}, u32[]{:S(2)}) %collective-permute-start.8) | collective-permute-done | bytes 65568 | tf_op jit(solution)/shard_map/ppermute | solution.py:43
  44.2 0.0 collective-permute-done.7
  44.2 0.1 pad_maximum_fusion.1
  44.2 0.1 collective-permute-start.11
  44.4 1.4 %collective-permute-done.11 = f32[128,4,128]{2,1,0:T(4,128)S(1)} collective-permute-done((f32[128,4,128]{2,1,0:T(4,128)S(1)}, f32[128,4,128]{2,1,0:T(4,128)S(1)}, u32[]{:S(2)}, u32[]{:S(2)}) %collective-permute-start.11) | collective-permute-done | bytes 262176 | tf_op jit(solution)/shard_map/ppermute | solution.py:22
  45.9 25.8 %force_sweep.1 = f32[3,16,128]{2,1,0:T(8,128)} custom-call(s32[48,128]{1,0:T(8,128)S(1)} %get-tuple-element.14.refs_0_, f32[288,8,128]{2,1,0:T(8,128)S(1)} %constant_dynamic-update-slice_fusion.2.refs_1_, f32[288,4,128]{2,1,0:T(4,128)S(1)} %constant_dynamic-update-slice_fusion.11.refs_2_, f32[16,31,8,128]{3,2,1,0:T(8,128)S(1)} %get-tuple-element.16.refs_3_, ...), custom_call_target="tpu_custom_call" | custom-call | tf_op jit(solution)/shard_map/force_sweep/pallas_call | solution.py:384
  (15 shorter events, 0.3 us)
Async XLA Ops:
  0.6 0.7 copy-start
  2.3 1.6 %collective-permute-start = (f32[16,8,128]{2,1,0:T(8,128)S(1)}, f32[16,8,128]{2,1,0:T(8,128)S(1)}, u32[]{:S(2)}, u32[]{:S(2)}) collective-permute-start(f32[16,8,128]{2,1,0:T(8,128)S(1)} %get-tuple-element.11), channel_id=1, source_target_pairs={{0,1},{1,0},{2,3},{3,2},{4,5},{5,4},{6,7},{7,6},{8,9},{9,8},{10,11... | collective-permute-start | bytes 196616 | tf_op jit(solution)/shard_map/ppermute | solution.py:22
  3.9 4.7 %collective-permute-start.4 = (f32[32,8,128]{2,1,0:T(8,128)S(1)}, f32[32,8,128]{2,1,0:T(8,128)S(1)}, u32[]{:S(2)}, u32[]{:S(2)}) collective-permute-start(f32[32,8,128]{2,1,0:T(8,128)S(1)} %get-tuple-element.18.after_ref), channel_id=1, source_target_pairs={{8,0},{0,1},{10,2},{2,3},{12,4},{4,5},{14,6},{6,7},{16,8},{1,9},{1... | collective-permute-start | bytes 393224 | tf_op jit(solution)/shard_map/ppermute | solution.py:43
  5.2 5.1 %collective-permute-start.3 = (f32[32,8,128]{2,1,0:T(8,128)S(1)}, f32[32,8,128]{2,1,0:T(8,128)S(1)}, u32[]{:S(2)}, u32[]{:S(2)}) collective-permute-start(f32[32,8,128]{2,1,0:T(8,128)S(1)} %get-tuple-element.18.after_ref), channel_id=1, source_target_pairs={{6,0},{0,1},{8,2},{2,3},{10,4},{4,5},{12,6},{1,7},{14,8},{3,9},{16... | collective-permute-start | bytes 393224 | tf_op jit(solution)/shard_map/ppermute | solution.py:43
  7.4 7.8 %collective-permute-start.2 = (f32[32,8,128]{2,1,0:T(8,128)S(1)}, f32[32,8,128]{2,1,0:T(8,128)S(1)}, u32[]{:S(2)}, u32[]{:S(2)}) collective-permute-start(f32[32,8,128]{2,1,0:T(8,128)S(1)} %get-tuple-element.18.after_ref), channel_id=1, source_target_pairs={{4,0},{0,1},{6,2},{2,3},{8,4},{1,5},{10,6},{3,7},{12,8},{5,9},{14,... | collective-permute-start | bytes 393224 | tf_op jit(solution)/shard_map/ppermute | solution.py:43
  8.7 6.6 %collective-permute-start.1 = (f32[32,8,128]{2,1,0:T(8,128)S(1)}, f32[32,8,128]{2,1,0:T(8,128)S(1)}, u32[]{:S(2)}, u32[]{:S(2)}) collective-permute-start(f32[32,8,128]{2,1,0:T(8,128)S(1)} %get-tuple-element.18.after_ref), channel_id=1, source_target_pairs={{2,0},{0,1},{4,2},{1,3},{6,4},{3,5},{8,6},{5,7},{10,8},{7,9},{12,1... | collective-permute-start | bytes 393224 | tf_op jit(solution)/shard_map/ppermute | solution.py:43
  15.3 4.1 %collective-permute-start.5 = (f32[128,8,128]{2,1,0:T(8,128)S(1)}, f32[128,8,128]{2,1,0:T(8,128)S(1)}, u32[]{:S(2)}, u32[]{:S(2)}) collective-permute-start(f32[128,8,128]{2,1,0:T(8,128)S(1)} %pad_maximum_fusion), channel_id=1, source_target_pairs={{0,1},{1,0},{2,3},{3,2},{4,5},{5,4},{6,7},{7,6},{8,9},{9,8},{10,11... | collective-permute-start | bytes 1572872 | tf_op jit(solution)/shard_map/ppermute | solution.py:22
  35.5 1.3 %collective-permute-start.6 = (f32[16,4,128]{2,1,0:T(4,128)S(1)}, f32[16,4,128]{2,1,0:T(4,128)S(1)}, u32[]{:S(2)}, u32[]{:S(2)}) collective-permute-start(f32[16,4,128]{2,1,0:T(4,128)S(1)} %get-tuple-element.15), channel_id=1, source_target_pairs={{0,1},{1,0},{2,3},{3,2},{4,5},{5,4},{6,7},{7,6},{8,9},{9,8},{10,11... | collective-permute-start | bytes 98312 | tf_op jit(solution)/shard_map/ppermute | solution.py:22
  36.8 5.2 %collective-permute-start.10 = (f32[32,4,128]{2,1,0:T(4,128)S(1)}, f32[32,4,128]{2,1,0:T(4,128)S(1)}, u32[]{:S(2)}, u32[]{:S(2)}) collective-permute-start(f32[32,4,128]{2,1,0:T(4,128)S(1)} %get-tuple-element.22.after_ref), channel_id=1, source_target_pairs={{8,0},{0,1},{10,2},{2,3},{12,4},{4,5},{14,6},{6,7},{16,8},{1,9},{1... | collective-permute-start | bytes 196616 | tf_op jit(solution)/shard_map/ppermute | solution.py:43
  36.8 5.1 %collective-permute-start.9 = (f32[32,4,128]{2,1,0:T(4,128)S(1)}, f32[32,4,128]{2,1,0:T(4,128)S(1)}, u32[]{:S(2)}, u32[]{:S(2)}) collective-permute-start(f32[32,4,128]{2,1,0:T(4,128)S(1)} %get-tuple-element.22.after_ref), channel_id=1, source_target_pairs={{6,0},{0,1},{8,2},{2,3},{10,4},{4,5},{12,6},{1,7},{14,8},{3,9},{16... | collective-permute-start | bytes 196616 | tf_op jit(solution)/shard_map/ppermute | solution.py:43
  39.0 5.2 %collective-permute-start.8 = (f32[32,4,128]{2,1,0:T(4,128)S(1)}, f32[32,4,128]{2,1,0:T(4,128)S(1)}, u32[]{:S(2)}, u32[]{:S(2)}) collective-permute-start(f32[32,4,128]{2,1,0:T(4,128)S(1)} %get-tuple-element.22.after_ref), channel_id=1, source_target_pairs={{4,0},{0,1},{6,2},{2,3},{8,4},{1,5},{10,6},{3,7},{12,8},{5,9},{14,... | collective-permute-start | bytes 196616 | tf_op jit(solution)/shard_map/ppermute | solution.py:43
  39.0 5.2 %collective-permute-start.7 = (f32[32,4,128]{2,1,0:T(4,128)S(1)}, f32[32,4,128]{2,1,0:T(4,128)S(1)}, u32[]{:S(2)}, u32[]{:S(2)}) collective-permute-start(f32[32,4,128]{2,1,0:T(4,128)S(1)} %get-tuple-element.22.after_ref), channel_id=1, source_target_pairs={{2,0},{0,1},{4,2},{1,3},{6,4},{3,5},{8,6},{5,7},{10,8},{7,9},{12,1... | collective-permute-start | bytes 196616 | tf_op jit(solution)/shard_map/ppermute | solution.py:43
  44.2 1.6 %collective-permute-start.11 = (f32[128,4,128]{2,1,0:T(4,128)S(1)}, f32[128,4,128]{2,1,0:T(4,128)S(1)}, u32[]{:S(2)}, u32[]{:S(2)}) collective-permute-start(f32[128,4,128]{2,1,0:T(4,128)S(1)} %pad_maximum_fusion.1), channel_id=1, source_target_pairs={{0,1},{1,0},{2,3},{3,2},{4,5},{5,4},{6,7},{7,6},{8,9},{9,8},{10,11... | collective-permute-start | bytes 786440 | tf_op jit(solution)/shard_map/ppermute | solution.py:22

commit v3 on v2

--- a/solution.py
+++ b/solution.py
@@ -63,7 +63,7 @@
     for entry in range(entries):
         turn = index_ref[2 * local_cells + cell, entry]
         following = index_ref[local_cells + cell, entry + 1]
-        rolled = pltpu.roll(lift(table[index_ref[cell, entry]]), turn, 1)
+        rolled = pltpu.roll(lift(table(index_ref[cell, entry])), turn, 1)
         merged = jnp.where(lane >= turn, rolled, held)
         pack[tile] = merged
         held = jnp.where(following > tile, rolled, merged)
@@ -80,7 +80,7 @@
     return 128 * tiles + index_ref[2 * local_cells + cell, entry + 1] - index_ref[2 * local_cells + cell, entry]
 
 
-def each_group(count, tile_count, body, finish, zeros):
+def each_group(most_rows, count, tile_count, body, finish, zeros):
     fours = lax.shift_right_logical(tile_count + 1, 2)
     twos = jnp.where(tile_count > 4 * fours, 1, 0)
 
@@ -94,11 +94,10 @@
 
     start = jnp.int32(0)
     eights = lax.shift_right_logical(count + 7, 3)
-    for rows, groups in (
-        (32, lax.shift_right_logical(eights, 2)),
-        (16, lax.bitwise_and(lax.shift_right_logical(eights, 1), 1)),
-        (8, lax.bitwise_and(eights, 1)),
-    ):
+    rows = most_rows
+    while rows >= 8:
+        groups = lax.shift_right_logical(eights, (rows // 8).bit_length() - 1)
+        groups = groups if rows == most_rows else lax.bitwise_and(groups, 1)
 
         def several(group, carry, start=start, rows=rows):
             per_group(start + group * rows, rows)
@@ -106,6 +105,7 @@
 
         lax.fori_loop(0, groups, several, 0)
         start = start + groups * rows
+        rows //= 2
 
 
 def row_sums(sums, local_cells):
@@ -150,7 +150,7 @@
     lax.fori_loop(0, spread_ref.shape[0] // 2, per_pair, 0)
 
 
-def find_partners(padded_ref, table_ref, code_ref, listed_ref, found_ref, columns):
+def find_partners(padded_ref, table_ref, code_ref, ids_ref, listed_ref, found_ref, columns):
     chips = lax.axis_size("curve")
     local_cells = padded_ref.shape[0]
     reach = reach_of(local_cells)
@@ -158,27 +158,29 @@
     inner = lax.broadcasted_iota(jnp.int32, (8, LANES), 0)
     starts = window_starts(lax.axis_index("curve"), lax.axis_index("group"), local_cells, reach)
     groups = []
-    for first in range(0, table_ref.shape[0], 8):
+    for first in range(0, table_ref.shape[0] // 8, 8):
         start, where = starts[first // local_cells]
         span = slice(first, first + 8)
-        lists = table_ref[span, 7, :].astype(jnp.int32)
+        lists = table_ref[pl.ds(8 * first + 7, 8, stride=8), :].astype(jnp.int32)
         real = (where >= 0) & (where < chips)
         count = lax.bitwise_and(lists, 255)
         code_ref[span, :] = jnp.where(real, (inner + first) * 256 + count, 0).astype(jnp.float32)
         listed_ref[span, :] = (lax.shift_right_logical(lists, 8) - 1).astype(jnp.float32)
-        groups.append((span, start + first % local_cells))
+        ids_ref[span, :] = (inner + (start + first % local_cells)).astype(jnp.float32)
+        groups.append(span)
     own_start = starts[0][0]
 
     def per_cell(cell, carry):
         own = own_start + cell
         row = padded_ref[pl.ds(cell, 1), :]
-        wanted = jnp.where(lane == columns, own, jnp.where(row >= 0, row, -(1 << 20)))
+        wanted = jnp.where(lane == columns, own, jnp.where(row >= 0, row, -(1 << 20))).astype(jnp.float32)
+        own = own.astype(jnp.float32)
         ahead = jnp.zeros((8, LANES), jnp.float32)
         behind = jnp.zeros((8, LANES), jnp.float32)
-        for span, start in groups:
+        for span in groups:
             code = code_ref[span, :]
-            ahead = jnp.maximum(ahead, jnp.where(inner == wanted - start, code, 0.0))
-            behind = jnp.maximum(behind, jnp.where(listed_ref[span, :] == own.astype(jnp.float32), code, 0.0))
+            ahead = jnp.maximum(ahead, jnp.where(ids_ref[span, :] == wanted, code, 0.0))
+            behind = jnp.maximum(behind, jnp.where(listed_ref[span, :] == own, code, 0.0))
         ahead = jnp.max(ahead, axis=0, keepdims=True)
         behind = pltpu.roll(jnp.max(behind, axis=0, keepdims=True), columns + 1, 1)
         found_ref[pl.ds(cell, 1), :] = jnp.where(lane <= columns, ahead, behind).astype(jnp.int32)
@@ -199,16 +201,17 @@
 
 def density_kernel(
     padded_ref, table_ref, own_ref, spread_ref,
-    out_ref, sent_ref, state_ref, pack_ref, index_ref, sums_ref, code_ref, listed_ref, found_ref, *, columns,
+    out_ref, sent_ref, state_ref, pack_ref, index_ref, sums_ref, code_ref, ids_ref, listed_ref, found_ref, *, columns,
 ):
     local_cells = out_ref.shape[0]
     entries = 2 * columns + 1
-    find_partners(padded_ref, table_ref, code_ref, listed_ref, found_ref, columns)
+    find_partners(padded_ref, table_ref, code_ref, ids_ref, listed_ref, found_ref, columns)
     pltpu.sync_copy(found_ref, index_ref)
 
     def per_cell(cell, carry):
         tile_count = pack_sources(
-            cell, local_cells, index_ref, entries, table_ref, lambda held: held, pack_ref.at[cell], 2
+            cell, local_cells, index_ref, entries,
+            lambda row: table_ref[pl.ds(pl.multiple_of(8 * row, 8), 8), :], lambda held: held, pack_ref.at[cell], 2,
         )
         count = count_of(cell, local_cells, index_ref, columns)
 
@@ -233,12 +236,12 @@
         def finish(span, total):
             sums_ref[cell, span, :] = total
 
-        each_group(count, tile_count, body, finish, lambda rows: jnp.zeros((rows, LANES), jnp.float32))
+        each_group(64, count, tile_count, body, finish, lambda rows: jnp.zeros((rows, LANES), jnp.float32))
         return carry
 
     lax.fori_loop(0, local_cells, per_cell, 0)
     raw = row_sums(sums_ref, local_cells)
-    masses = jnp.concatenate([table_ref[cell, 3:4, :] for cell in range(local_cells)], axis=0)
+    masses = table_ref[pl.ds(3, local_cells, stride=8), :]
     smooth = jnp.concatenate([own_ref[cell, 10:11, :] for cell in range(local_cells)], axis=0)
     entropy = jnp.concatenate([own_ref[cell, 11:12, :] for cell in range(local_cells)], axis=0)
     held = masses > 0.0
@@ -275,7 +278,7 @@
 
     def per_cell(cell, carry):
         tile_count = pack_sources(
-            cell, local_cells, index_ref, entries, state_ref, with_sound, state_pack_ref, 2
+            cell, local_cells, index_ref, entries, lambda row: state_ref[row], with_sound, state_pack_ref, 2
         )
         count = count_of(cell, local_cells, index_ref, columns)
 
@@ -310,12 +313,12 @@
                 sums_ref[d, cell, span, :] = total[d]
 
         each_group(
-            count, tile_count, body, finish, lambda rows: (jnp.zeros((rows, LANES), jnp.float32),) * 3
+            32, count, tile_count, body, finish, lambda rows: (jnp.zeros((rows, LANES), jnp.float32),) * 3
         )
         return carry
 
     lax.fori_loop(0, local_cells, per_cell, 0)
-    held = jnp.concatenate([table_ref[cell, 3:4, :] for cell in range(local_cells)], axis=0) > 0.0
+    held = table_ref[pl.ds(3, local_cells, stride=8), :] > 0.0
     for d in range(3):
         out_ref[d] = jnp.where(held, row_sums(sums_ref.at[d], local_cells), 0.0)
 
@@ -344,7 +347,7 @@
         out_specs=(whole, whole, whole),
         name="prepare",
         compiler_params=pltpu.CompilerParams(vmem_limit_bytes=ROOM),
-    )(counts, off_chip(particles), off_chip(pair_lists))
+    )(off_chip(counts), off_chip(particles), off_chip(pair_lists))
 
     def spread(rows, channels, after):
         return pl.pallas_call(
@@ -357,9 +360,9 @@
         )(rows, after)
 
     window, own_spread = surround(sent, lambda after: spread(own, 10, after))
-    table = on_chip(window)
+    table = on_chip(window.reshape(-1, slots))
     most_tiles = 2 * columns + 5
-    rows = table.shape[0]
+    rows = window.shape[0]
     density, thermal, state, packed, index = pl.pallas_call(
         lambda *refs: density_kernel(*refs, columns=columns),
         out_shape=(
@@ -373,6 +376,7 @@
         out_specs=(whole, whole, whole, whole, scalars),
         scratch_shapes=[
             floats(local_cells, LANES, LANES),
+            floats(rows, LANES),
             floats(rows, LANES),
             floats(rows, LANES),
             pltpu.VMEM((3 * local_cells, LANES), jnp.int32),

time: 71.9 us -> 70.2 us (0.976)
  Pallas kernels: 49.4 us -> 48.3 us
    pallas_call x1, Pallas kernels: 16 us -> 14.9 us  [per_device(): pl.pallas_call(lambda *refs: density_kernel(*refs, columns=columns), out_...]
where the time goes in v3:
time: 70.2 us; the launch traced here: 70 us
  Pallas kernels  48.3 us (69%)
  waiting for transfers between devices  12.2 us (17%)
  starting transfers between devices  8.37 us (12%)
  between operations  0.79 us (1%)
    pallas_call x1, Pallas kernels, per_device(): pl.pallas_call(lambda *refs: force_kernel(*refs, columns=columns), out_sh...  25.8 us
    pallas_call x1, Pallas kernels, per_device(): pl.pallas_call(lambda *refs: density_kernel(*refs, columns=columns), out_...  14.9 us
    ppermute x8, waiting for transfers between devices, surround(): fetched.append(lax.ppermute(chip_block, AXES, route_of(chips, k)))  8.85 us
    ppermute x8, starting transfers between devices, surround(): fetched.append(lax.ppermute(chip_block, AXES, route_of(chips, k)))  7.29 us
    pallas_call x2, Pallas kernels, spread(): pl.pallas_call(spread_kernel, out_shape=floats(local_cells, channels, LAN...  6.63 us
    ppermute x4, waiting for transfers between devices, swap_cores(): return lax.ppermute(block, 'group', [(0, 1), (1, 0)])  3.4 us
  transfers between devices with their start and end apart: 12, of which 6 were waited for; matrix products, arithmetic and copies ran while one was open for 0% of the time, Pallas kernels for 9%

profile of v3, /device:TPU:13, one launch (start us, length us, event | category | flops | bytes accessed | tf_op | source)
XLA Modules:
  0.0 70.0 jit_solution(1610523244508013181)
XLA Ops:
  0.6 1.0 %prepare.1 = (f32[16,8,128]{2,1,0:T(8,128)S(1)}, s32[16,128]{1,0:T(8,128)S(1)}, f32[16,16,128]{2,1,0:T(8,128)S(1)}) custom-call(s32[16]{0:T(128)} %counts_ref.1, f32[9,16,128]{2,1,0:T(8,128)} %bitcast.5, s32[16,13]{1,0:T(8,128)} %lists_ref.1), custom_call_target="tpu_custom_call" | custom-call | tf_op jit(solution)/shard_map/prepare/pallas_call | solution.py:343
  1.6 0.7 %collective-permute-start = (f32[16,8,128]{2,1,0:T(8,128)S(1)}, f32[16,8,128]{2,1,0:T(8,128)S(1)}, u32[]{:S(2)}, u32[]{:S(2)}) collective-permute-start(f32[16,8,128]{2,1,0:T(8,128)S(1)} %get-tuple-element.11), channel_id=1, source_target_pairs={{0,1},{1,0},{2,3},{3,2},{4,5},{5,4},{6,7},{7,6},{8,9},{9,8},{10,11... | collective-permute-start | bytes 196616 | tf_op jit(solution)/shard_map/ppermute | solution.py:22
  2.4 0.9 %collective-permute-done = f32[16,8,128]{2,1,0:T(8,128)S(1)} collective-permute-done((f32[16,8,128]{2,1,0:T(8,128)S(1)}, f32[16,8,128]{2,1,0:T(8,128)S(1)}, u32[]{:S(2)}, u32[]{:S(2)}) %collective-permute-start) | collective-permute-done | bytes 65568 | tf_op jit(solution)/shard_map/ppermute | solution.py:22
  3.3 1.3 %collective-permute-start.4 = (f32[32,8,128]{2,1,0:T(8,128)S(1)}, f32[32,8,128]{2,1,0:T(8,128)S(1)}, u32[]{:S(2)}, u32[]{:S(2)}) collective-permute-start(f32[32,8,128]{2,1,0:T(8,128)S(1)} %get-tuple-element.18.after_ref), channel_id=1, source_target_pairs={{8,0},{0,1},{10,2},{2,3},{12,4},{4,5},{14,6},{6,7},{16,8},{1,9},{1... | collective-permute-start | bytes 393224 | tf_op jit(solution)/shard_map/ppermute | solution.py:43
  4.6 2.2 %collective-permute-start.3 = (f32[32,8,128]{2,1,0:T(8,128)S(1)}, f32[32,8,128]{2,1,0:T(8,128)S(1)}, u32[]{:S(2)}, u32[]{:S(2)}) collective-permute-start(f32[32,8,128]{2,1,0:T(8,128)S(1)} %get-tuple-element.18.after_ref), channel_id=1, source_target_pairs={{6,0},{0,1},{8,2},{2,3},{10,4},{4,5},{12,6},{1,7},{14,8},{3,9},{16... | collective-permute-start | bytes 393224 | tf_op jit(solution)/shard_map/ppermute | solution.py:43
  6.8 1.2 %collective-permute-start.2 = (f32[32,8,128]{2,1,0:T(8,128)S(1)}, f32[32,8,128]{2,1,0:T(8,128)S(1)}, u32[]{:S(2)}, u32[]{:S(2)}) collective-permute-start(f32[32,8,128]{2,1,0:T(8,128)S(1)} %get-tuple-element.18.after_ref), channel_id=1, source_target_pairs={{4,0},{0,1},{6,2},{2,3},{8,4},{1,5},{10,6},{3,7},{12,8},{5,9},{14,... | collective-permute-start | bytes 393224 | tf_op jit(solution)/shard_map/ppermute | solution.py:43
  8.0 0.0 collective-permute-start.1
  8.0 0.0 collective-permute-done.4
  8.0 1.7 %collective-permute-done.3 = f32[32,8,128]{2,1,0:T(8,128)S(1)} collective-permute-done((f32[32,8,128]{2,1,0:T(8,128)S(1)}, f32[32,8,128]{2,1,0:T(8,128)S(1)}, u32[]{:S(2)}, u32[]{:S(2)}) %collective-permute-start.3) | collective-permute-done | bytes 131104 | tf_op jit(solution)/shard_map/ppermute | solution.py:43
  9.7 4.9 %collective-permute-done.2 = f32[32,8,128]{2,1,0:T(8,128)S(1)} collective-permute-done((f32[32,8,128]{2,1,0:T(8,128)S(1)}, f32[32,8,128]{2,1,0:T(8,128)S(1)}, u32[]{:S(2)}, u32[]{:S(2)}) %collective-permute-start.2) | collective-permute-done | bytes 131104 | tf_op jit(solution)/shard_map/ppermute | solution.py:43
  14.6 0.0 collective-permute-done.1
  14.6 0.1 collective-permute-start.5
  14.7 4.0 %spread.2.refs_3_.refs_4_ = f32[16,10,128,128]{3,2,1,0:T(8,128)S(1)} custom-call(f32[16,16,128]{2,1,0:T(8,128)S(1)} %get-tuple-element.12.rows_ref.refs_2_, f32[32,8,128]{2,1,0:T(8,128)S(1)} %get-tuple-element.18.after_ref), custom_call_target="tpu_custom_call" | custom-call | tf_op jit(solution)/shard_map/spread/pallas_call | solution.py:353
  18.8 0.0 collective-permute-done.5
  18.8 14.9 %density_sweep.1 = (f32[16,128]{1,0:T(8,128)}, f32[16,4,128]{2,1,0:T(4,128)S(1)}, f32[16,8,128]{2,1,0:T(8,128)S(1)}, f32[16,31,8,128]{3,2,1,0:T(8,128)S(1)}, s32[48,128]{1,0:T(8,128)S(1)}) custom-call(s32[16,128]{1,0:T(8,128)S(1)} %get-tuple-element.10.refs_0_, f32[2304,128]{1,0:T(8,128)S(1)} %bitcast.3, ...), custom_call_target="tpu_custom_call" | custom-call | tf_op jit(solution)/shard_map/density_sweep/pallas_call | solution.py:366
  33.7 0.2 collective-permute-start.6
  33.9 1.1 %collective-permute-done.6 = f32[16,4,128]{2,1,0:T(4,128)S(1)} collective-permute-done((f32[16,4,128]{2,1,0:T(4,128)S(1)}, f32[16,4,128]{2,1,0:T(4,128)S(1)}, u32[]{:S(2)}, u32[]{:S(2)}) %collective-permute-start.6) | collective-permute-done | bytes 32800 | tf_op jit(solution)/shard_map/ppermute | solution.py:22
  35.0 0.0 collective-permute-start.10
  35.1 2.3 %collective-permute-start.9 = (f32[32,4,128]{2,1,0:T(4,128)S(1)}, f32[32,4,128]{2,1,0:T(4,128)S(1)}, u32[]{:S(2)}, u32[]{:S(2)}) collective-permute-start(f32[32,4,128]{2,1,0:T(4,128)S(1)} %get-tuple-element.22.after_ref), channel_id=1, source_target_pairs={{6,0},{0,1},{8,2},{2,3},{10,4},{4,5},{12,6},{1,7},{14,8},{3,9},{16... | collective-permute-start | bytes 196616 | tf_op jit(solution)/shard_map/ppermute | solution.py:43
  37.3 0.0 collective-permute-start.8
  37.3 0.3 collective-permute-start.7
  37.6 2.7 %spread.3.refs_5_ = f32[16,3,128,128]{3,2,1,0:T(8,128)S(1)} custom-call(f32[16,8,128]{2,1,0:T(8,128)S(1)} %get-tuple-element.17.rows_ref, f32[32,4,128]{2,1,0:T(4,128)S(1)} %get-tuple-element.22.after_ref), custom_call_target="tpu_custom_call" | custom-call | tf_op jit(solution)/shard_map/spread/pallas_call | solution.py:353
  40.3 0.0 collective-permute-done.10
  40.3 0.0 collective-permute-done.9
  40.3 2.2 %collective-permute-done.8 = f32[32,4,128]{2,1,0:T(4,128)S(1)} collective-permute-done((f32[32,4,128]{2,1,0:T(4,128)S(1)}, f32[32,4,128]{2,1,0:T(4,128)S(1)}, u32[]{:S(2)}, u32[]{:S(2)}) %collective-permute-start.8) | collective-permute-done | bytes 65568 | tf_op jit(solution)/shard_map/ppermute | solution.py:43
  42.5 0.0 collective-permute-done.7
  42.5 0.1 pad_maximum_fusion.1
  42.6 0.1 collective-permute-start.11
  42.8 1.4 %collective-permute-done.11 = f32[128,4,128]{2,1,0:T(4,128)S(1)} collective-permute-done((f32[128,4,128]{2,1,0:T(4,128)S(1)}, f32[128,4,128]{2,1,0:T(4,128)S(1)}, u32[]{:S(2)}, u32[]{:S(2)}) %collective-permute-start.11) | collective-permute-done | bytes 262176 | tf_op jit(solution)/shard_map/ppermute | solution.py:22
  44.2 25.8 %force_sweep.1 = f32[3,16,128]{2,1,0:T(8,128)} custom-call(s32[48,128]{1,0:T(8,128)S(1)} %get-tuple-element.14.refs_0_, f32[2304,128]{1,0:T(8,128)S(1)} %bitcast.4, f32[288,4,128]{2,1,0:T(4,128)S(1)} %constant_dynamic-update-slice_fusion.11.refs_2_, f32[16,31,8,128]{3,2,1,0:T(8,128)S(1)} %get-tuple-element.16.refs_3_, ...), custom_call_target="tpu_custom_call" | custom-call | tf_op jit(solution)/shard_map/force_sweep/pallas_call | solution.py:388
  (15 shorter events, 0.3 us)
Async XLA Ops:
  1.6 1.6 %collective-permute-start = (f32[16,8,128]{2,1,0:T(8,128)S(1)}, f32[16,8,128]{2,1,0:T(8,128)S(1)}, u32[]{:S(2)}, u32[]{:S(2)}) collective-permute-start(f32[16,8,128]{2,1,0:T(8,128)S(1)} %get-tuple-element.11), channel_id=1, source_target_pairs={{0,1},{1,0},{2,3},{3,2},{4,5},{5,4},{6,7},{7,6},{8,9},{9,8},{10,11... | collective-permute-start | bytes 196616 | tf_op jit(solution)/shard_map/ppermute | solution.py:22
  3.3 4.7 %collective-permute-start.4 = (f32[32,8,128]{2,1,0:T(8,128)S(1)}, f32[32,8,128]{2,1,0:T(8,128)S(1)}, u32[]{:S(2)}, u32[]{:S(2)}) collective-permute-start(f32[32,8,128]{2,1,0:T(8,128)S(1)} %get-tuple-element.18.after_ref), channel_id=1, source_target_pairs={{8,0},{0,1},{10,2},{2,3},{12,4},{4,5},{14,6},{6,7},{16,8},{1,9},{1... | collective-permute-start | bytes 393224 | tf_op jit(solution)/shard_map/ppermute | solution.py:43
  4.6 5.1 %collective-permute-start.3 = (f32[32,8,128]{2,1,0:T(8,128)S(1)}, f32[32,8,128]{2,1,0:T(8,128)S(1)}, u32[]{:S(2)}, u32[]{:S(2)}) collective-permute-start(f32[32,8,128]{2,1,0:T(8,128)S(1)} %get-tuple-element.18.after_ref), channel_id=1, source_target_pairs={{6,0},{0,1},{8,2},{2,3},{10,4},{4,5},{12,6},{1,7},{14,8},{3,9},{16... | collective-permute-start | bytes 393224 | tf_op jit(solution)/shard_map/ppermute | solution.py:43
  6.8 7.8 %collective-permute-start.2 = (f32[32,8,128]{2,1,0:T(8,128)S(1)}, f32[32,8,128]{2,1,0:T(8,128)S(1)}, u32[]{:S(2)}, u32[]{:S(2)}) collective-permute-start(f32[32,8,128]{2,1,0:T(8,128)S(1)} %get-tuple-element.18.after_ref), channel_id=1, source_target_pairs={{4,0},{0,1},{6,2},{2,3},{8,4},{1,5},{10,6},{3,7},{12,8},{5,9},{14,... | collective-permute-start | bytes 393224 | tf_op jit(solution)/shard_map/ppermute | solution.py:43
  8.0 6.6 %collective-permute-start.1 = (f32[32,8,128]{2,1,0:T(8,128)S(1)}, f32[32,8,128]{2,1,0:T(8,128)S(1)}, u32[]{:S(2)}, u32[]{:S(2)}) collective-permute-start(f32[32,8,128]{2,1,0:T(8,128)S(1)} %get-tuple-element.18.after_ref), channel_id=1, source_target_pairs={{2,0},{0,1},{4,2},{1,3},{6,4},{3,5},{8,6},{5,7},{10,8},{7,9},{12,1... | collective-permute-start | bytes 393224 | tf_op jit(solution)/shard_map/ppermute | solution.py:43
  14.6 4.1 %collective-permute-start.5 = (f32[128,8,128]{2,1,0:T(8,128)S(1)}, f32[128,8,128]{2,1,0:T(8,128)S(1)}, u32[]{:S(2)}, u32[]{:S(2)}) collective-permute-start(f32[128,8,128]{2,1,0:T(8,128)S(1)} %pad_maximum_fusion), channel_id=1, source_target_pairs={{0,1},{1,0},{2,3},{3,2},{4,5},{5,4},{6,7},{7,6},{8,9},{9,8},{10,11... | collective-permute-start | bytes 1572872 | tf_op jit(solution)/shard_map/ppermute | solution.py:22
  33.7 1.3 %collective-permute-start.6 = (f32[16,4,128]{2,1,0:T(4,128)S(1)}, f32[16,4,128]{2,1,0:T(4,128)S(1)}, u32[]{:S(2)}, u32[]{:S(2)}) collective-permute-start(f32[16,4,128]{2,1,0:T(4,128)S(1)} %get-tuple-element.15), channel_id=1, source_target_pairs={{0,1},{1,0},{2,3},{3,2},{4,5},{5,4},{6,7},{7,6},{8,9},{9,8},{10,11... | collective-permute-start | bytes 98312 | tf_op jit(solution)/shard_map/ppermute | solution.py:22
  35.0 5.3 %collective-permute-start.10 = (f32[32,4,128]{2,1,0:T(4,128)S(1)}, f32[32,4,128]{2,1,0:T(4,128)S(1)}, u32[]{:S(2)}, u32[]{:S(2)}) collective-permute-start(f32[32,4,128]{2,1,0:T(4,128)S(1)} %get-tuple-element.22.after_ref), channel_id=1, source_target_pairs={{8,0},{0,1},{10,2},{2,3},{12,4},{4,5},{14,6},{6,7},{16,8},{1,9},{1... | collective-permute-start | bytes 196616 | tf_op jit(solution)/shard_map/ppermute | solution.py:43
  35.1 5.2 %collective-permute-start.9 = (f32[32,4,128]{2,1,0:T(4,128)S(1)}, f32[32,4,128]{2,1,0:T(4,128)S(1)}, u32[]{:S(2)}, u32[]{:S(2)}) collective-permute-start(f32[32,4,128]{2,1,0:T(4,128)S(1)} %get-tuple-element.22.after_ref), channel_id=1, source_target_pairs={{6,0},{0,1},{8,2},{2,3},{10,4},{4,5},{12,6},{1,7},{14,8},{3,9},{16... | collective-permute-start | bytes 196616 | tf_op jit(solution)/shard_map/ppermute | solution.py:43
  37.3 5.2 %collective-permute-start.8 = (f32[32,4,128]{2,1,0:T(4,128)S(1)}, f32[32,4,128]{2,1,0:T(4,128)S(1)}, u32[]{:S(2)}, u32[]{:S(2)}) collective-permute-start(f32[32,4,128]{2,1,0:T(4,128)S(1)} %get-tuple-element.22.after_ref), channel_id=1, source_target_pairs={{4,0},{0,1},{6,2},{2,3},{8,4},{1,5},{10,6},{3,7},{12,8},{5,9},{14,... | collective-permute-start | bytes 196616 | tf_op jit(solution)/shard_map/ppermute | solution.py:43
  37.3 5.2 %collective-permute-start.7 = (f32[32,4,128]{2,1,0:T(4,128)S(1)}, f32[32,4,128]{2,1,0:T(4,128)S(1)}, u32[]{:S(2)}, u32[]{:S(2)}) collective-permute-start(f32[32,4,128]{2,1,0:T(4,128)S(1)} %get-tuple-element.22.after_ref), channel_id=1, source_target_pairs={{2,0},{0,1},{4,2},{1,3},{6,4},{3,5},{8,6},{5,7},{10,8},{7,9},{12,1... | collective-permute-start | bytes 196616 | tf_op jit(solution)/shard_map/ppermute | solution.py:43
  42.6 1.6 %collective-permute-start.11 = (f32[128,4,128]{2,1,0:T(4,128)S(1)}, f32[128,4,128]{2,1,0:T(4,128)S(1)}, u32[]{:S(2)}, u32[]{:S(2)}) collective-permute-start(f32[128,4,128]{2,1,0:T(4,128)S(1)} %pad_maximum_fusion.1), channel_id=1, source_target_pairs={{0,1},{1,0},{2,3},{3,2},{4,5},{5,4},{6,7},{7,6},{8,9},{9,8},{10,11... | collective-permute-start | bytes 786440 | tf_op jit(solution)/shard_map/ppermute | solution.py:22
